TPU v7x, 32 devices: a whole 2x2x4 slice. The times are simulated.
32 devices in a mesh: data: 2 (over x), expert: 16 (over z, y, core).
Axes of the slice: x: 2, y: 2, z: 4, core: 2. Of those that a mesh axis runs over, the one named last changes fastest.
Arguments:
- x_a: bfloat16 [8192, 1024], P(('data', 'expert')), parts along dimension 0
- x_b: bfloat16 [8192, 1024], P(('data', 'expert')), parts along dimension 0
- dy_b: bfloat16 [8192, 1024], P(('data', 'expert')), parts along dimension 0
- eid_a: int32 [8192, 8], P(('data', 'expert')), parts along dimension 0
- slot_a: int32 [8192, 8], P(('data', 'expert')), parts along dimension 0
- gate_a: bfloat16 [8192, 8], P(('data', 'expert')), parts along dimension 0
- eid_b: int32 [8192, 8], P(('data', 'expert')), parts along dimension 0
- slot_b: int32 [8192, 8], P(('data', 'expert')), parts along dimension 0
- gate_b: bfloat16 [8192, 8], P(('data', 'expert')), parts along dimension 0
- u_b: bfloat16 [64, 2048, 1024], P(('data', 'expert')), parts along dimension 0
- norm_1: bfloat16 [1024], replicated
- norm_2: bfloat16 [1024], replicated
- w_q: bfloat16 [1024, 16, 64], replicated
- w_k: bfloat16 [1024, 8, 64], replicated
- w_v: bfloat16 [1024, 8, 64], replicated
- w_o: bfloat16 [16, 64, 1024], replicated
- w_1: bfloat16 [32, 1024, 512], P('expert')
- w_2: bfloat16 [32, 512, 1024], P('expert')
- w_3: bfloat16 [32, 1024, 512], P('expert')
Outputs:
- output 1: bfloat16 [8192, 1024], P(('data', 'expert')), parts along dimension 0
- output 2: bfloat16 [8192, 1024], P(('data', 'expert')), parts along dimension 0
- output 3: float32 [64, 1024, 512], P(('data', 'expert')), parts along dimension 0
- output 4: float32 [64, 512, 1024], P(('data', 'expert')), parts along dimension 0
- output 5: float32 [64, 1024, 512], P(('data', 'expert')), parts along dimension 0
- output 6: float32 [32, 1024, 16, 64], P(('data', 'expert')), parts along dimension 0
- output 7: float32 [32, 1024, 8, 64], P(('data', 'expert')), parts along dimension 0
- output 8: float32 [32, 1024, 8, 64], P(('data', 'expert')), parts along dimension 0
- output 9: float32 [32, 16, 64, 1024], P(('data', 'expert')), parts along dimension 0
- output 10: float32 [32, 1024], P(('data', 'expert')), parts along dimension 0
- output 11: float32 [32, 1024], P(('data', 'expert')), parts along dimension 0
There are 2 independent parts. A program takes and returns all parts, laid end to end along the dimension named above; an argument that names none is the same for every part.
All inputs are finite; a program needn't handle non-finite values.
Results may differ from a plain program's by a relative error of at most 0.0176189.
Values are sent between devices in bfloat16 or wider.
A program may use at most 1 GiB of HBM per device.

v0:
```python
import jax
import jax.numpy as jnp
from jax import lax
from jax.sharding import PartitionSpec as P

NORM_EPS = 1e-6


def rms_norm(values, gain):
    wide = values.astype(jnp.float32)
    scaled = wide * lax.rsqrt(jnp.mean(wide * wide, axis=-1, keepdims=True) + NORM_EPS)
    return (scaled * gain.astype(jnp.float32)).astype(jnp.bfloat16)


def add_rows(first, second):
    return (first.astype(jnp.float32) + second.astype(jnp.float32)).astype(jnp.bfloat16)


def attn_out(x_rows, norm_gain, w_q, w_k, w_v, w_o):
    tokens = x_rows.shape[0]
    heads = w_q.shape[1]
    kv_heads = w_k.shape[1]
    head_dim = w_q.shape[2]
    normed = rms_norm(x_rows, norm_gain)
    query = jnp.einsum('td,dhe->the', normed, w_q, preferred_element_type=jnp.float32).astype(jnp.bfloat16)
    query = query.reshape(tokens, kv_heads, heads // kv_heads, head_dim)
    key_proj = jnp.einsum('td,dge->tge', normed, w_k, preferred_element_type=jnp.float32).astype(jnp.bfloat16)
    val_proj = jnp.einsum('td,dge->tge', normed, w_v, preferred_element_type=jnp.float32).astype(jnp.bfloat16)
    scores = jnp.einsum('tgre,mge->grtm', query, key_proj, preferred_element_type=jnp.float32) * head_dim ** -0.5
    causal = jnp.arange(tokens)[:, None] >= jnp.arange(tokens)[None, :]
    scores = jnp.where(causal, scores, -1e30)
    probs = jax.nn.softmax(scores, axis=-1).astype(jnp.bfloat16)
    context = jnp.einsum('grtm,mge->tgre', probs, val_proj, preferred_element_type=jnp.float32).astype(jnp.bfloat16)
    context = context.reshape(tokens, heads, head_dim)
    return jnp.einsum('the,hed->td', context, w_o, preferred_element_type=jnp.float32).astype(jnp.bfloat16)


def dispatch(row_vals, expert_ids, slot_ids, experts, capacity):
    safe_slots = jnp.where(slot_ids >= 0, slot_ids, capacity)
    values = jnp.broadcast_to(row_vals, expert_ids.shape + (row_vals.shape[-1],))
    return jnp.zeros((experts, capacity, row_vals.shape[-1]), jnp.bfloat16).at[expert_ids, safe_slots].set(values, mode='drop')


def pick_rows(buf, expert_ids, slot_ids):
    safe_slots = jnp.where(slot_ids >= 0, slot_ids, buf.shape[1])
    return buf.at[expert_ids, safe_slots].get(mode='fill', fill_value=0)


def device_backward(x_dev, dy_dev, du_dev, norm_1, norm_2, w_q, w_k, w_v, w_o):
    attn_val, attn_pull = jax.vjp(attn_out, x_dev, norm_1, w_q, w_k, w_v, w_o)
    h_dev = add_rows(x_dev, attn_val)
    _, norm_pull = jax.vjp(rms_norm, h_dev, norm_2)
    dh_norm, grad_n2 = norm_pull(du_dev)
    dh_dev = add_rows(dy_dev, dh_norm)
    grad_x, grad_n1, grad_q, grad_k, grad_v, grad_o = attn_pull(dh_dev)
    return (add_rows(dh_dev, grad_x), grad_q.astype(jnp.float32), grad_k.astype(jnp.float32), grad_v.astype(jnp.float32), grad_o.astype(jnp.float32), grad_n1.astype(jnp.float32), grad_n2.astype(jnp.float32))


def solution(mesh):
    group = mesh.shape['expert']

    def local_step(x_a, x_b, dy_b, eid_a, slot_a, gate_a, eid_b, slot_b, gate_b, u_b, norm_1, norm_2, w_q, w_k, w_v, w_o, w_1, w_2, w_3):
        local_experts = w_1.shape[0]
        experts = local_experts * group
        capacity = u_b.shape[1] // group
        model_dim = x_a.shape[1]

        h_a = add_rows(x_a, attn_out(x_a, norm_1, w_q, w_k, w_v, w_o))
        u_a = rms_norm(h_a, norm_2)
        send_a = dispatch(u_a[:, None, :], eid_a, slot_a, experts, capacity).reshape(group, local_experts, capacity, model_dim)
        recv_a = lax.all_to_all(send_a, 'expert', 0, 0, tiled=True)
        act_1 = jnp.einsum('pecd,edf->pecf', recv_a, w_1, preferred_element_type=jnp.float32).astype(jnp.bfloat16).astype(jnp.float32)
        act_3 = jnp.einsum('pecd,edf->pecf', recv_a, w_3, preferred_element_type=jnp.float32).astype(jnp.bfloat16).astype(jnp.float32)
        hidden = (act_1 * jax.nn.sigmoid(act_1) * act_3).astype(jnp.bfloat16)
        out_a = jnp.einsum('pecf,efd->pecd', hidden, w_2, preferred_element_type=jnp.float32).astype(jnp.bfloat16)
        back_a = lax.all_to_all(out_a, 'expert', 0, 0, tiled=True).reshape(experts, capacity, model_dim)
        mixed = jnp.einsum('tk,tkd->td', gate_a, pick_rows(back_a, eid_a, slot_a), preferred_element_type=jnp.float32)
        y_a = (h_a.astype(jnp.float32) + mixed).astype(jnp.bfloat16)

        grad_rows = gate_b[:, :, None] * dy_b[:, None, :]
        send_b = dispatch(grad_rows, eid_b, slot_b, experts, capacity).reshape(group, local_experts, capacity, model_dim)
        d_out = lax.all_to_all(send_b, 'expert', 0, 0, tiled=True)
        saved = u_b.reshape(local_experts, group, capacity, model_dim)
        pre_1 = jnp.einsum('epcd,edf->pecf', saved, w_1, preferred_element_type=jnp.float32).astype(jnp.bfloat16).astype(jnp.float32)
        pre_3 = jnp.einsum('epcd,edf->pecf', saved, w_3, preferred_element_type=jnp.float32).astype(jnp.bfloat16).astype(jnp.float32)
        sigma = jax.nn.sigmoid(pre_1)
        silu_1 = pre_1 * sigma
        hid_b = (silu_1 * pre_3).astype(jnp.bfloat16)
        grad_w2 = jnp.einsum('pecf,pecd->efd', hid_b, d_out, preferred_element_type=jnp.float32)
        grad_hid = jnp.einsum('pecd,efd->pecf', d_out, w_2, preferred_element_type=jnp.float32).astype(jnp.bfloat16).astype(jnp.float32)
        grad_a1 = (grad_hid * pre_3 * sigma * (1.0 + pre_1 * (1.0 - sigma))).astype(jnp.bfloat16)
        grad_a3 = (grad_hid * silu_1).astype(jnp.bfloat16)
        grad_w1 = jnp.einsum('epcd,pecf->edf', saved, grad_a1, preferred_element_type=jnp.float32)
        grad_w3 = jnp.einsum('epcd,pecf->edf', saved, grad_a3, preferred_element_type=jnp.float32)
        grad_in = (jnp.einsum('pecf,edf->pecd', grad_a1, w_1, preferred_element_type=jnp.float32) + jnp.einsum('pecf,edf->pecd', grad_a3, w_3, preferred_element_type=jnp.float32)).astype(jnp.bfloat16)
        back_b = lax.all_to_all(grad_in, 'expert', 0, 0, tiled=True).reshape(experts, capacity, model_dim)
        du_rows = jnp.sum(pick_rows(back_b, eid_b, slot_b), axis=1, dtype=jnp.float32).astype(jnp.bfloat16)
        dx_b, g_q, g_k, g_v, g_o, g_n1, g_n2 = device_backward(x_b, dy_b, du_rows, norm_1, norm_2, w_q, w_k, w_v, w_o)
        return (y_a, dx_b, grad_w1, grad_w2, grad_w3, g_q[None], g_k[None], g_v[None], g_o[None], g_n1[None], g_n2[None])

    row_spec = P(('data', 'expert'), None)
    cube_spec = P(('data', 'expert'), None, None)
    quad_spec = P(('data', 'expert'), None, None, None)
    expert_spec = P('expert', None, None)
    in_specs = (row_spec, row_spec, row_spec, row_spec, row_spec, row_spec, row_spec, row_spec, row_spec, cube_spec, P(), P(), P(), P(), P(), P(), expert_spec, expert_spec, expert_spec)
    out_specs = (row_spec, row_spec, cube_spec, cube_spec, cube_spec, quad_spec, quad_spec, quad_spec, quad_spec, row_spec, row_spec)
    return jax.shard_map(local_step, mesh=mesh, in_specs=in_specs, out_specs=out_specs, check_vma=False)
```

profile of v0, /device:TPU:13, one launch (start us, length us, event | category | flops | bytes accessed | tf_op | source)
XLA Modules:
  0.0 974.8 jit_solution(2242091550709486704)
XLA Ops:
  6.7 15.2 %scatter_custom_fusion.1 = bf16[4096,1024]{1,0:T(8,128)(2,1)} fusion(s32[2048]{0:T(1024)S(1)} %reshape.195, bf16[]{:T(256)} %constant.40.clone.1, bf16[256,1024]{1,0:T(8,128)(2,1)} %param.21, bf16[256,8]{1,0:T(8,128)(2,1)S(1)} %copy.71), kind=kCustom, calls=%fused_computation.50 | custom fusion | flops 2097152 | bytes 8978434
  22.0 6.9 all-to-all-start.2
  28.9 9.6 convolution_convert_fusion
  38.5 9.7 convolution_convert_fusion.1
  48.2 163.1 %all-to-all-done.2 = bf16[16,2,128,1024]{3,2,1,0:T(8,128)(2,1)} async-done(((bf16[16,2,128,1024]{3,2,1,0:T(8,128)(2,1)}), bf16[16,2,128,1024]{3,2,1,0:T(8,128)(2,1)}, u32[]{:S(2)}, u32[]{:S(2)}) %all-to-all-start.2) | async-done | bytes 8388640 | tf_op jit(solution)/shard_map/all_to_all | solution.py:82
  211.3 10.7 %fusion.47 = bf16[2,16,128,512]{3,2,1,0:T(8,128)(2,1)} fusion(bf16[16,2,128,1024]{3,2,1,0:T(8,128)(2,1)} %all-to-all-done.2, bf16[2,512,1024]{2,1,0:T(8,128)(2,1)} %param.36), kind=kOutput, calls=%fused_computation.72 | convolution fusion | flops 4297064448 | bytes 14680064 | tf_op jit(solution)/shard_map/pecd,efd->pecf/dot_general | solution.py:90
  222.0 15.8 %fusion.64 = f32[2,16,128,1024]{3,2,1,0:T(8,128)} fusion(bf16[2,1024,512]{2,1,0:T(8,128)(2,1)S(1)} %copy-done, bf16[2,512,16,128]{1,3,2,0:T(8,128)(2,1)S(1)} %copy-done.44, bf16[2,512,16,128]{1,3,2,0:T(8,128)(2,1)} %convolution_convert_fusion.1, bf16[2,16,128,512]{3,2,1,0:T(8,128)(2,1)} %fusion.47), kind=kOutput, calls=%fused_computation.83 | convolution fusion | flops 4322230272 | bytes 31457280 | tf_op jit(solution)/shard_map/pecf,edf->pecd/dot_general | solution.py:95
  237.8 23.5 %fusion.1 = bf16[16,2,128,1024]{3,2,0,1:T(8,128)(2,1)} fusion(f32[2,16,128,1024]{3,2,1,0:T(8,128)} %fusion.64, bf16[2,1024,512]{2,1,0:T(8,128)(2,1)S(1)} %copy-done.38, bf16[2,16,128,512]{3,2,1,0:T(8,128)(2,1)} %fusion.47, bf16[2,512,16,128]{1,3,2,0:T(8,128)(2,1)} %convolution_convert_fusion), kind=kOutput, calls=%fused_computation.6 | convolution fusion | flops 4320133120 | bytes 35651584 | tf_op jit(solution)/shard_map/pecf,edf->pecd/dot_general | solution.py:95
  261.3 8.2 copy.77
  302.3 154.7 %all-to-all-done.3 = bf16[16,2,128,1024]{3,2,1,0:T(8,128)(2,1)} async-done(((bf16[16,2,128,1024]{3,2,1,0:T(8,128)(2,1)}), bf16[16,2,128,1024]{3,2,1,0:T(8,128)(2,1)}, u32[]{:S(2)}, u32[]{:S(2)}) %all-to-all-start.3) | async-done | bytes 8388640 | tf_op jit(solution)/shard_map/all_to_all | solution.py:96
  457.0 40.8 %gather_fusion.1 = bf16[2048,1024]{1,0:T(8,128)(2,1)} fusion(bf16[32,128,1024]{2,1,0:T(8,128)(2,1)} %bitcast.46, s32[2048]{0:T(1024)S(1)} %reshape.183), kind=kCustom, calls=%fused_computation.1 | custom fusion | bytes 8404992 | tf_op jit(solution)/shard_map/gather | solution.py:46
  505.1 15.0 %scatter_custom_fusion = bf16[4096,1024]{1,0:T(8,128)(2,1)} fusion(s32[2048]{0:T(1024)S(1)} %reshape.189, bf16[]{:T(256)} %constant.40.clone.1, bf16[256,1024]{1,0:T(8,128)(2,1)} %get-tuple-element.57), kind=kCustom, calls=%fused_computation.54 | custom fusion | bytes 8912898
  520.0 187.3 %all_to_all.20 = bf16[16,2,128,1024]{3,2,1,0:T(8,128)(2,1)S(1)} all-to-all(bf16[16,2,128,1024]{3,2,1,0:T(8,128)(2,1)} %bitcast.387), channel_id=1, replica_groups=mesh['data'=2,'expert'=16] {'expert'}, dimensions={0} | all-to-all | bytes 16777216 | tf_op jit(solution)/shard_map/all_to_all | solution.py:71
  710.6 6.2 fusion.19
  716.7 15.3 %convert_bitcast_fusion = bf16[16,2,128,1024]{3,2,0,1:T(8,128)(2,1)} fusion(bf16[2,16,128,512]{3,2,1,0:T(8,128)(2,1)} %fusion.19, bf16[16,2,128,1024]{3,2,1,0:T(8,128)(2,1)} %copy-done.7, bf16[2,1024,512]{2,1,0:T(8,128)(2,1)S(1)} %copy-done, bf16[2,512,1024]{2,1,0:T(8,128)(2,1)} %param.36), kind=kOutput, calls=%fused_computation.29 | convolution fusion | flops 8613003264 | bytes 25165824 | tf_op jit(solution)/shard_map/pecf,efd->pecd/dot_general | solution.py:75
  732.0 8.2 copy.67
  740.2 6.1 all-to-all-start.1
  747.0 14.8 %convolution_bitcast_fusion.1 = f32[2,1024,512]{1,2,0:T(8,128)} fusion(bf16[2,16,128,1024]{3,2,1,0:T(8,128)(2,1)} %bitcast.415, bf16[2,512,16,128]{1,3,2,0:T(8,128)(2,1)} %convolution_convert_fusion, bf16[2,512,16,128]{1,3,2,0:T(8,128)(2,1)} %convolution_convert_fusion.1, bf16[2,16,128,512]{3,2,1,0:T(8,128)(2,1)} %fusion.47), kind=kOutput, calls=%fused_computation.76 | convolution fusion | flops 4322230272 | bytes 25165824 | tf_op jit(solution)/shard_map/epcd,pecf->edf/dot_general | solution.py:93
  761.8 5.4 copy.85
  767.2 12.6 %convolution_bitcast_fusion = f32[2,1024,512]{1,2,0:T(8,128)} fusion(bf16[2,16,128,1024]{3,2,1,0:T(8,128)(2,1)} %bitcast.416, bf16[2,16,128,512]{3,2,1,0:T(8,128)(2,1)} %fusion.47, bf16[2,512,16,128]{1,3,2,0:T(8,128)(2,1)} %convolution_convert_fusion), kind=kOutput, calls=%fused_computation.75 | convolution fusion | flops 4311744512 | bytes 20971520 | tf_op jit(solution)/shard_map/epcd,pecf->edf/dot_general | solution.py:94
  779.8 5.6 copy.86
  785.4 12.8 %fusion.55 = f32[2,512,1024]{2,1,0:T(8,128)} fusion(bf16[16,2,128,1024]{3,2,1,0:T(8,128)(2,1)} %all-to-all-done.2, bf16[2,512,16,128]{1,3,2,0:T(8,128)(2,1)} %convolution_convert_fusion.1, bf16[2,512,16,128]{1,3,2,0:T(8,128)(2,1)} %convolution_convert_fusion), kind=kOutput, calls=%fused_computation.74 | convolution fusion | flops 4311744512 | bytes 20971520 | tf_op jit(solution)/shard_map/pecf,pecd->efd/dot_general | solution.py:89
  818.9 109.9 %all-to-all-done.1 = bf16[16,2,128,1024]{3,2,1,0:T(8,128)(2,1)} async-done(((bf16[16,2,128,1024]{3,2,1,0:T(8,128)(2,1)}), bf16[16,2,128,1024]{3,2,1,0:T(8,128)(2,1)}, u32[]{:S(2)}, u32[]{:S(2)}) %all-to-all-start.1) | async-done | bytes 8388640 | tf_op jit(solution)/shard_map/all_to_all | solution.py:76
  928.8 40.9 %gather_fusion = bf16[2048,1024]{1,0:T(8,128)(2,1)} fusion(bf16[32,128,1024]{2,1,0:T(8,128)(2,1)} %bitcast.28, s32[2048]{0:T(1024)S(1)} %reshape.177), kind=kCustom, calls=%fused_computation | custom fusion | bytes 8404992 | tf_op jit(solution)/shard_map/gather | solution.py:46
  (163 shorter events, 74.9 us)
Async XLA Ops:
  0.6 28.2 %copy-start = (bf16[2,1024,512]{2,1,0:T(8,128)(2,1)S(1)}, bf16[2,1024,512]{2,1,0:T(8,128)(2,1)}, u32[]{:S(2)}) copy-start(bf16[2,1024,512]{2,1,0:T(8,128)(2,1)} %param.35) | copy-start | bytes 6291460
  22.0 189.3 %all-to-all-start.2 = ((bf16[16,2,128,1024]{3,2,1,0:T(8,128)(2,1)}), bf16[16,2,128,1024]{3,2,1,0:T(8,128)(2,1)}, u32[]{:S(2)}, u32[]{:S(2)}) async-start(bf16[16,2,128,1024]{3,2,1,0:T(8,128)(2,1)} %bitcast.386), calls=%async_computation.2 | async-start | bytes 16777216 | tf_op jit(solution)/shard_map/all_to_all | solution.py:82
  28.9 9.6 copy-start.37
  211.3 10.7 %copy-start.44 = (bf16[2,512,16,128]{1,3,2,0:T(8,128)(2,1)S(1)}, bf16[2,512,16,128]{1,3,2,0:T(8,128)(2,1)}, u32[]{:S(2)}) copy-start(bf16[2,512,16,128]{1,3,2,0:T(8,128)(2,1)} %convolution_convert_fusion) | copy-start | bytes 12582916
  222.0 15.8 %copy-start.38 = (bf16[2,1024,512]{2,1,0:T(8,128)(2,1)S(1)}, bf16[2,1024,512]{2,1,0:T(8,128)(2,1)}, u32[]{:S(2)}) copy-start(bf16[2,1024,512]{2,1,0:T(8,128)(2,1)} %param.37) | copy-start | bytes 6291460
  269.5 5.7 copy-start.6
  269.5 5.9 copy-start.17
  269.5 187.5 %all-to-all-start.3 = ((bf16[16,2,128,1024]{3,2,1,0:T(8,128)(2,1)}), bf16[16,2,128,1024]{3,2,1,0:T(8,128)(2,1)}, u32[]{:S(2)}, u32[]{:S(2)}) async-start(bf16[16,2,128,1024]{3,2,1,0:T(8,128)(2,1)} %copy.77), calls=%async_computation.3 | async-start | bytes 16777216 | tf_op jit(solution)/shard_map/all_to_all | solution.py:96
  275.1 5.8 copy-start.40
  275.4 6.9 copy-start.31
  275.6 6.7 copy-start.29
  275.6 6.7 copy-start.15
  279.6 6.4 copy-start.23
  297.4 204.8 %copy-start.10 = (bf16[256,1024]{1,0:T(8,128)(2,1)}, bf16[256,1024]{1,0:T(8,128)(2,1)S(1)}, u32[]{:S(2)}) copy-start(bf16[256,1024]{1,0:T(8,128)(2,1)S(1)} %get-tuple-element.63) | copy-start | bytes 1572868
  520.0 190.5 %copy-start.39 = (bf16[2,1024,512]{2,1,0:T(8,128)(2,1)S(1)}, bf16[2,1024,512]{2,1,0:T(8,128)(2,1)}, u32[]{:S(2)}) copy-start(bf16[2,1024,512]{2,1,0:T(8,128)(2,1)} %param.37) | copy-start | bytes 6291460
  740.2 6.1 copy-start.27
  740.2 6.1 copy-start.28
  740.2 6.4 copy-start.33
  740.2 6.6 copy-start.34
  740.2 188.6 %all-to-all-start.1 = ((bf16[16,2,128,1024]{3,2,1,0:T(8,128)(2,1)}), bf16[16,2,128,1024]{3,2,1,0:T(8,128)(2,1)}, u32[]{:S(2)}, u32[]{:S(2)}) async-start(bf16[16,2,128,1024]{3,2,1,0:T(8,128)(2,1)} %copy.67), calls=%async_computation.1 | async-start | bytes 16777216 | tf_op jit(solution)/shard_map/all_to_all | solution.py:76
  785.4 12.8 %copy-start.9 = (bf16[16,64,1024]{2,1,0:T(8,128)(2,1)S(1)}, bf16[16,64,1024]{2,1,0:T(8,128)(2,1)}, u32[]{:S(2)}) copy-start(bf16[16,64,1024]{2,1,0:T(8,128)(2,1)} %param.34) | copy-start | bytes 6291460
  785.4 13.5 %copy-start.3 = (f32[8,256,256,2]{2,1,3,0:T(8,128)S(1)}, f32[8,256,256,2]{2,1,3,0:T(8,128)}, u32[]{:S(2)}) copy-start(f32[8,256,256,2]{2,1,3,0:T(8,128)} %copy-done.2) | copy-start | bytes 12582916
  785.4 13.5 %copy-start.24 = (f32[256,512]{0,1:S(1)}, f32[256,512]{0,1}, u32[]{:S(2)}) copy-start(f32[256,512]{0,1} %copy-done.23) | copy-start | bytes 1572868
  928.8 45.6 %copy-start.1 = (bf16[2,1024,512]{2,1,0:T(8,128)(2,1)S(1)}, bf16[2,1024,512]{2,1,0:T(8,128)(2,1)}, u32[]{:S(2)}) copy-start(bf16[2,1024,512]{2,1,0:T(8,128)(2,1)} %param.35) | copy-start | bytes 6291460
  (24 other events, 76.3 us)
where the time goes:
time: 982 us; the launch traced here: 975 us
  waiting for transfers between devices  428 us (44%)
  blocking collectives  187 us (19%)
  matrix products  169 us (17%)
  local copies, waits for them, and re-layouts  131 us (13%)
  other arithmetic  40.3 us (4%)
  starting transfers between devices  17.9 us (2%)
    all_to_all x1, blocking collectives, local_step(): recv_a = lax.all_to_all(send_a, 'expert', 0, 0, tiled=True)  187 us
    all_to_all x1, waiting for transfers between devices, local_step(): d_out = lax.all_to_all(send_b, 'expert', 0, 0, tiled=True)  163 us
    all_to_all x1, waiting for transfers between devices, local_step(): lax.all_to_all(grad_in, 'expert', 0, 0, tiled=True)  155 us
    all_to_all x1, waiting for transfers between devices, local_step(): lax.all_to_all(out_a, 'expert', 0, 0, tiled=True)  110 us
    gather x2, local copies, waits for them, and re-layouts, pick_rows(): return buf.at[expert_ids, safe_slots].get(mode='fill', fill_value=0)  81.7 us
    unnamed x99, local copies, waits for them, and re-layouts  32.3 us
    dot_general x1, matrix products, local_step(): jnp.einsum('pecf,edf->pecd', grad_a3, w_3, preferred_element_type=jnp.flo...  23.5 us
  transfers between devices with their start and end apart: 3, of which 3 were waited for; matrix products, arithmetic and copies ran while one was open for 12% of the time, Pallas kernels for 0%

commit v1 on v0

v1 whole, which is shorter than its diff:
```python
import jax
import jax.numpy as jnp
from jax import lax
from jax.sharding import PartitionSpec as P

NORM_EPS = 1e-6


def rms_norm(values, gain):
    wide = values.astype(jnp.float32)
    scaled = wide * lax.rsqrt(jnp.mean(wide * wide, axis=-1, keepdims=True) + NORM_EPS)
    return (scaled * gain.astype(jnp.float32)).astype(jnp.bfloat16)


def add_rows(first, second):
    return (first.astype(jnp.float32) + second.astype(jnp.float32)).astype(jnp.bfloat16)


def attn_out(x_rows, norm_gain, w_q, w_k, w_v, w_o):
    tokens = x_rows.shape[0]
    heads = w_q.shape[1]
    kv_heads = w_k.shape[1]
    head_dim = w_q.shape[2]
    normed = rms_norm(x_rows, norm_gain)
    query = jnp.einsum('td,dhe->the', normed, w_q, preferred_element_type=jnp.float32).astype(jnp.bfloat16)
    query = query.reshape(tokens, kv_heads, heads // kv_heads, head_dim)
    key_proj = jnp.einsum('td,dge->tge', normed, w_k, preferred_element_type=jnp.float32).astype(jnp.bfloat16)
    val_proj = jnp.einsum('td,dge->tge', normed, w_v, preferred_element_type=jnp.float32).astype(jnp.bfloat16)
    scores = jnp.einsum('tgre,mge->grtm', query, key_proj, preferred_element_type=jnp.float32) * head_dim ** -0.5
    causal = jnp.arange(tokens)[:, None] >= jnp.arange(tokens)[None, :]
    scores = jnp.where(causal, scores, -1e30)
    probs = jax.nn.softmax(scores, axis=-1).astype(jnp.bfloat16)
    context = jnp.einsum('grtm,mge->tgre', probs, val_proj, preferred_element_type=jnp.float32).astype(jnp.bfloat16)
    context = context.reshape(tokens, heads, head_dim)
    return jnp.einsum('the,hed->td', context, w_o, preferred_element_type=jnp.float32).astype(jnp.bfloat16)


def routing_table(expert_ids, slot_ids, gates, experts):
    hit = (expert_ids[:, :, None] == jnp.arange(experts)[None, None, :]) & (slot_ids >= 0)[:, :, None]
    slots = jnp.sum(jnp.where(hit, slot_ids[:, :, None] + 1, 0), axis=1) - 1
    weights = jnp.sum(jnp.where(hit, gates.astype(jnp.float32)[:, :, None], 0.0), axis=1)
    return slots.astype(jnp.bfloat16), weights.astype(jnp.bfloat16)


def device_backward(x_dev, dy_dev, du_dev, norm_1, norm_2, w_q, w_k, w_v, w_o):
    attn_val, attn_pull = jax.vjp(attn_out, x_dev, norm_1, w_q, w_k, w_v, w_o)
    h_dev = add_rows(x_dev, attn_val)
    _, norm_pull = jax.vjp(rms_norm, h_dev, norm_2)
    dh_norm, grad_n2 = norm_pull(du_dev)
    dh_dev = add_rows(dy_dev, dh_norm)
    grad_x, grad_n1, grad_q, grad_k, grad_v, grad_o = attn_pull(dh_dev)
    return (add_rows(dh_dev, grad_x), grad_q.astype(jnp.float32), grad_k.astype(jnp.float32), grad_v.astype(jnp.float32), grad_o.astype(jnp.float32), grad_n1.astype(jnp.float32), grad_n2.astype(jnp.float32))


def solution(mesh):
    group = mesh.shape['expert']

    def local_step(x_a, x_b, dy_b, eid_a, slot_a, gate_a, eid_b, slot_b, gate_b, u_b, norm_1, norm_2, w_q, w_k, w_v, w_o, w_1, w_2, w_3):
        local_experts = w_1.shape[0]
        experts = local_experts * group
        capacity = u_b.shape[1] // group
        model_dim = x_a.shape[1]

        tokens = x_a.shape[0]
        me = lax.axis_index('expert')
        meta = jnp.concatenate(routing_table(eid_b, slot_b, gate_b, experts) + routing_table(eid_a, slot_a, gate_a, experts), axis=1)
        meta_all = lax.all_gather(meta, 'expert', axis=0)
        dy_all = lax.all_gather(dy_b, 'expert', axis=0)
        h_a = add_rows(x_a, attn_out(x_a, norm_1, w_q, w_k, w_v, w_o))
        u_a = rms_norm(h_a, norm_2)
        u_all = lax.all_gather(u_a, 'expert', axis=0)

        fields = meta_all.reshape(group, tokens, 4, group, local_experts)
        mine = lax.dynamic_index_in_dim(fields, me, 3, keepdims=False)
        slot_of_b, gate_of_b, slot_of_a, gate_of_a = mine[:, :, 0], mine[:, :, 1], mine[:, :, 2], mine[:, :, 3]
        columns = jnp.arange(capacity).astype(jnp.bfloat16)

        def place(slots, weights):
            return jnp.where(slots[:, :, :, None] == columns, weights[:, :, :, None], jnp.zeros((), jnp.bfloat16))

        ones = jnp.ones_like(gate_of_b)
        gated_b = place(slot_of_b, gate_of_b)
        plain_b = place(slot_of_b, ones)
        gated_a = place(slot_of_a, gate_of_a)
        plain_a = place(slot_of_a, ones)

        saved = u_b.reshape(local_experts, group, capacity, model_dim)
        pre_1 = jnp.einsum('epcd,edf->epcf', saved, w_1, preferred_element_type=jnp.float32).astype(jnp.bfloat16).astype(jnp.float32)
        pre_3 = jnp.einsum('epcd,edf->epcf', saved, w_3, preferred_element_type=jnp.float32).astype(jnp.bfloat16).astype(jnp.float32)
        sigma = jax.nn.sigmoid(pre_1)
        silu_1 = pre_1 * sigma
        hid_b = (silu_1 * pre_3).astype(jnp.bfloat16)
        d_out = jnp.einsum('ptec,ptd->epcd', gated_b, dy_all, preferred_element_type=jnp.float32).astype(jnp.bfloat16)
        grad_hid = jnp.einsum('epcd,efd->epcf', d_out, w_2, preferred_element_type=jnp.float32).astype(jnp.bfloat16).astype(jnp.float32)
        grad_a1 = (grad_hid * pre_3 * sigma * (1.0 + pre_1 * (1.0 - sigma))).astype(jnp.bfloat16)
        grad_a3 = (grad_hid * silu_1).astype(jnp.bfloat16)
        grad_in = (jnp.einsum('epcf,edf->epcd', grad_a1, w_1, preferred_element_type=jnp.float32) + jnp.einsum('epcf,edf->epcd', grad_a3, w_3, preferred_element_type=jnp.float32)).astype(jnp.bfloat16)
        part_b = jnp.einsum('ptec,epcd->ptd', plain_b, grad_in, preferred_element_type=jnp.float32).reshape(group * tokens, model_dim)
        du_rows = lax.psum_scatter(part_b, 'expert', scatter_dimension=0, tiled=True).astype(jnp.bfloat16)
        grad_w2 = jnp.einsum('epcf,epcd->efd', hid_b, d_out, preferred_element_type=jnp.float32)
        grad_w1 = jnp.einsum('epcd,epcf->edf', saved, grad_a1, preferred_element_type=jnp.float32)
        grad_w3 = jnp.einsum('epcd,epcf->edf', saved, grad_a3, preferred_element_type=jnp.float32)

        recv_a = jnp.einsum('ptec,ptd->epcd', plain_a, u_all, preferred_element_type=jnp.float32).astype(jnp.bfloat16)
        act_1 = jnp.einsum('epcd,edf->epcf', recv_a, w_1, preferred_element_type=jnp.float32).astype(jnp.bfloat16).astype(jnp.float32)
        act_3 = jnp.einsum('epcd,edf->epcf', recv_a, w_3, preferred_element_type=jnp.float32).astype(jnp.bfloat16).astype(jnp.float32)
        hidden = (act_1 * jax.nn.sigmoid(act_1) * act_3).astype(jnp.bfloat16)
        out_a = jnp.einsum('epcf,efd->epcd', hidden, w_2, preferred_element_type=jnp.float32).astype(jnp.bfloat16)
        part_a = jnp.einsum('ptec,epcd->ptd', gated_a, out_a, preferred_element_type=jnp.float32).reshape(group * tokens, model_dim)
        mixed = lax.psum_scatter(part_a, 'expert', scatter_dimension=0, tiled=True)
        y_a = (h_a.astype(jnp.float32) + mixed).astype(jnp.bfloat16)

        dx_b, g_q, g_k, g_v, g_o, g_n1, g_n2 = device_backward(x_b, dy_b, du_rows, norm_1, norm_2, w_q, w_k, w_v, w_o)
        return (y_a, dx_b, grad_w1, grad_w2, grad_w3, g_q[None], g_k[None], g_v[None], g_o[None], g_n1[None], g_n2[None])

    row_spec = P(('data', 'expert'), None)
    cube_spec = P(('data', 'expert'), None, None)
    quad_spec = P(('data', 'expert'), None, None, None)
    expert_spec = P('expert', None, None)
    in_specs = (row_spec, row_spec, row_spec, row_spec, row_spec, row_spec, row_spec, row_spec, row_spec, cube_spec, P(), P(), P(), P(), P(), P(), expert_spec, expert_spec, expert_spec)
    out_specs = (row_spec, row_spec, cube_spec, cube_spec, cube_spec, quad_spec, quad_spec, quad_spec, quad_spec, row_spec, row_spec)
    return jax.shard_map(local_step, mesh=mesh, in_specs=in_specs, out_specs=out_specs, check_vma=False)
```

time: 982 us -> 668 us (0.68)
  the two profiles are of different devices: /device:TPU:13 before, /device:TPU:0 now
where the time goes in v1:
time: 668 us; the launch traced here: 664 us
  waiting for transfers between devices  423 us (63%)
  matrix products  184 us (28%)
  other arithmetic  25.7 us (4%)
  local copies, waits for them, and re-layouts  15.1 us (2%)
  between operations  14.9 us (2%)
    reduce_scatter x1, waiting for transfers between devices, local_step(): lax.psum_scatter(part_b, 'expert', scatter_dimension=0, tiled=True)  148 us
    reduce_scatter x1, waiting for transfers between devices, local_step(): mixed = lax.psum_scatter(part_a, 'expert', scatter_dimension=0, tiled=True)  107 us
    all_gather x1, waiting for transfers between devices, local_step(): dy_all = lax.all_gather(dy_b, 'expert', axis=0)  75.4 us
    all_gather x1, waiting for transfers between devices, local_step(): u_all = lax.all_gather(u_a, 'expert', axis=0)  73.7 us
    all_gather x1, waiting for transfers between devices, local_step(): meta_all = lax.all_gather(meta, 'expert', axis=0)  18.5 us
    dot_general x1, matrix products, local_step(): jnp.einsum('epcd,efd->epcf', d_out, w_2, preferred_element_type=jnp.float32)  15.7 us
    unnamed x67, local copies, waits for them, and re-layouts  15 us
    dot_general x1, matrix products, local_step(): jnp.einsum('ptec,epcd->ptd', plain_b, grad_in, preferred_element_type=jnp...  14.4 us
  transfers between devices with their start and end apart: 5, of which 5 were waited for; matrix products, arithmetic and copies ran while one was open for 17% of the time, Pallas kernels for 0%

profile of v1, /device:TPU:0, one launch (start us, length us, event | category | flops | bytes accessed | tf_op | source)
XLA Modules:
  0.0 663.6 jit_solution(15301039187036213516)
XLA Ops:
  15.4 10.5 %convolution_convert_fusion = bf16[2,16,128,512]{3,2,1,0:T(8,128)(2,1)} fusion(bf16[2,16,128,1024]{3,2,1,0:T(8,128)(2,1)} %bitcast.335, bf16[2,1024,512]{2,1,0:T(8,128)(2,1)} %param.35), kind=kOutput, calls=%fused_computation.63 | convolution fusion | flops 4297064448 | bytes 14680064 | tf_op jit(solution)/shard_map/epcd,edf->epcf/dot_general | solution.py:88
  25.9 9.7 %convolution_convert_fusion.1 = bf16[2,16,128,512]{3,2,1,0:T(8,128)(2,1)} fusion(bf16[2,16,128,1024]{3,2,1,0:T(8,128)(2,1)} %bitcast.336, bf16[2,1024,512]{2,1,0:T(8,128)(2,1)S(1)} %copy-done), kind=kOutput, calls=%fused_computation.64 | convolution fusion | flops 4297064448 | bytes 14680064 | tf_op jit(solution)/shard_map/epcd,edf->epcf/dot_general | solution.py:89
  35.6 18.5 %all-gather.7.cloned.1.call-done = bf16[4096,128]{0,1:T(8,128)(2,1)} async-done(((bf16[256,128]{0,1:T(8,128)(2,1)}), bf16[4096,128]{0,1:T(8,128)(2,1)}) %all-gather.7.cloned.1.call-update) | async-done | bytes 1048592 | tf_op jit(solution)/shard_map/all_gather | solution.py:67
  55.7 75.4 %all-gather.11.cloned.1.call-done = bf16[4096,1024]{1,0:T(8,128)(2,1)} async-done(((bf16[256,1024]{1,0:T(8,128)(2,1)}), bf16[4096,1024]{1,0:T(8,128)(2,1)}) %all-gather.11.cloned.1.call-update) | async-done | bytes 8388624 | tf_op jit(solution)/shard_map/all_gather | solution.py:68
  131.1 6.9 %convert_bitcast_fusion = bf16[2,16,128,1024]{3,2,0,1:T(8,128)(2,1)S(1)} fusion(bf16[16,256,1024,1]{2,1,3,0:T(8,128)(2,1)} %bitcast.339, bf16[16,256,2]{1,2,0:T(2,128)(2,1)S(1)} %copy.109, bf16[16,256,2]{1,2,0:T(2,128)(2,1)S(1)} %copy.108, bf16[128]{0:T(256)(128)(2,1)S(1)} %iota_convert_fusion), kind=kOutput, calls=%fused_computation.23 | convolution fusion | flops 2153775104 | bytes 16810240 | tf_op jit(solution)/shard_map/ptec,ptd->epcd/dot_general | solution.py:93
  138.0 15.7 %fusion.5 = (bf16[2,16,128,512]{3,2,1,0:T(8,128)(2,1)}, bf16[2,16,128,512]{3,2,1,0:T(8,128)(2,1)}) fusion(bf16[2,16,128,512]{3,2,1,0:T(8,128)(2,1)} %convolution_convert_fusion, bf16[2,16,128,512]{3,2,1,0:T(8,128)(2,1)} %convolution_convert_fusion.1, bf16[2,512,1024]{2,1,0:T(8,128)(2,1)S(1)} %copy-done.26, ...), kind=kOutput, calls=%fused_computation.14 | convolution fusion | flops 4330618880 | bytes 27262976 | tf_op jit(solution)/shard_map/epcd,efd->epcf/dot_general | solution.py:94
  153.7 10.4 %fusion.34 = f32[2,16,128,1024]{3,2,0,1:T(8,128)} fusion(bf16[2,16,128,512]{3,2,1,0:T(8,128)(2,1)} %get-tuple-element.60, bf16[2,1024,512]{2,1,0:T(8,128)(2,1)S(1)} %copy-done.25), kind=kOutput, calls=%fused_computation.52 | convolution fusion | flops 4294967296 | bytes 23068672 | tf_op jit(solution)/shard_map/epcf,edf->epcd/dot_general | solution.py:97
  164.1 14.4 %fusion.55 = f32[16,256,1024,1]{2,1,3,0:T(8,128)} fusion(bf16[16,256,2]{1,2,0:T(2,128)(2,1)S(1)} %copy.108, bf16[128]{0:T(256)(128)(2,1)S(1)} %iota_convert_fusion, f32[2,16,128,1024]{3,2,0,1:T(8,128)} %fusion.34, bf16[2,16,128,512]{3,2,1,0:T(8,128)(2,1)} %get-tuple-element.59, bf16[2,1024,512]{2,1,0:T(8,128)(2,1)S(1)} %copy-done), kind=kOutput, calls=%fused_computation.69 | convolution fusion | flops 6452936704 | bytes 39862528 | tf_op jit(solution)/shard_map/ptec,epcd->ptd/dot_general | solution.py:98
  181.9 2.8 fusion.165
  193.7 4.7 fusion.183
  198.3 3.0 fusion.69
  204.5 147.9 %reduce-scatter.5.cloned.1.call-done = f32[256,1024]{1,0:T(8,128)} async-done(((f32[4096,1024]{1,0:T(8,128)}), f32[256,1024]{1,0:T(8,128)}) %reduce-scatter.5.cloned.1.call-update) | async-done | bytes 1048592 | tf_op jit(solution)/shard_map/reduce_scatter | solution.py:99
  354.2 2.9 add_convert_fusion.2
  357.7 73.7 %all-gather.9.cloned.1.call-done = bf16[4096,1024]{1,0:T(8,128)(2,1)} async-done(((bf16[256,1024]{1,0:T(8,128)(2,1)}), bf16[4096,1024]{1,0:T(8,128)(2,1)}) %all-gather.9.cloned.1.call-update) | async-done | bytes 8388624 | tf_op jit(solution)/shard_map/all_gather | solution.py:71
  431.4 11.8 %convert_bitcast_fusion.1 = bf16[2,16,128,1024]{2,3,0,1:T(8,128)(2,1)} fusion(bf16[16,256,1024,1]{2,1,3,0:T(8,128)(2,1)} %bitcast.340, bf16[128]{0:T(256)(128)(2,1)S(1)} %iota_convert_fusion, bf16[16,256,2]{1,2,0:T(2,128)(2,1)S(1)} %copy.102), kind=kOutput, calls=%fused_computation.26 | convolution fusion | flops 2155872256 | bytes 16793856 | tf_op jit(solution)/shard_map/ptec,ptd->epcd/dot_general | solution.py:104
  443.2 11.7 %fusion.17 = bf16[2,16,128,512]{3,2,1,0:T(8,128)(2,1)} fusion(bf16[2,16,128,1024]{2,3,0,1:T(8,128)(2,1)} %convert_bitcast_fusion.1, bf16[2,1024,512]{2,1,0:T(8,128)(2,1)S(1)} %copy-done), kind=kOutput, calls=%fused_computation.28 | convolution fusion | flops 4294967296 | bytes 14680064 | tf_op jit(solution)/shard_map/epcd,edf->epcf/dot_general | solution.py:106
  454.9 13.6 %fusion.16 = bf16[2,16,128,512]{3,2,1,0:T(8,128)(2,1)} fusion(bf16[2,16,128,512]{3,2,1,0:T(8,128)(2,1)} %fusion.17, bf16[2,16,128,1024]{2,3,0,1:T(8,128)(2,1)} %convert_bitcast_fusion.1, bf16[2,1024,512]{2,1,0:T(8,128)(2,1)} %param.35), kind=kOutput, calls=%fused_computation.27 | convolution fusion | flops 4313841664 | bytes 18874368 | tf_op jit(solution)/shard_map/epcd,edf->epcf/dot_general | solution.py:105
  468.5 11.9 %fusion.14 = f32[16,256,1024,1]{2,1,3,0:T(8,128)} fusion(bf16[2,16,128,512]{3,2,1,0:T(8,128)(2,1)} %fusion.16, bf16[2,512,1024]{2,1,0:T(8,128)(2,1)S(1)} %copy-done.27, bf16[16,256,2]{1,2,0:T(2,128)(2,1)S(1)} %copy.103, bf16[128]{0:T(256)(128)(2,1)S(1)} %iota_convert_fusion, bf16[16,256,2]{1,2,0:T(2,128)(2,1)S(1)} %copy.102), kind=kOutput, calls=%fused_computation.24 | convolution fusion | flops 6448742400 | bytes 23101696 | tf_op jit(solution)/shard_map/ptec,epcd->ptd/dot_general | solution.py:109
  480.5 11.2 %convolution_bitcast_fusion = f32[2,1024,512]{1,2,0:T(8,128)} fusion(bf16[2,16,128,512]{3,2,1,0:T(8,128)(2,1)} %get-tuple-element.59, bf16[2,16,128,1024]{3,2,1,0:T(8,128)(2,1)} %bitcast.337), kind=kOutput, calls=%fused_computation.67 | convolution fusion | flops 4294967296 | bytes 16777216 | tf_op jit(solution)/shard_map/epcd,epcf->edf/dot_general | solution.py:102
  491.7 5.4 copy.121
  497.1 11.2 %convolution_bitcast_fusion.1 = f32[2,1024,512]{1,2,0:T(8,128)} fusion(bf16[2,16,128,512]{3,2,1,0:T(8,128)(2,1)} %get-tuple-element.60, bf16[2,16,128,1024]{3,2,1,0:T(8,128)(2,1)} %bitcast.338), kind=kOutput, calls=%fused_computation.68 | convolution fusion | flops 4294967296 | bytes 16777216 | tf_op jit(solution)/shard_map/epcd,epcf->edf/dot_general | solution.py:101
  508.3 5.6 copy.120
  513.9 12.8 %fusion.46 = f32[2,512,1024]{2,1,0:T(8,128)} fusion(bf16[2,16,128,1024]{3,2,0,1:T(8,128)(2,1)} %copy-done.31, bf16[2,16,128,512]{3,2,1,0:T(8,128)(2,1)} %convolution_convert_fusion.1, bf16[2,16,128,512]{3,2,1,0:T(8,128)(2,1)} %convolution_convert_fusion), kind=kOutput, calls=%fused_computation.66 | convolution fusion | flops 4311744512 | bytes 20971520 | tf_op jit(solution)/shard_map/epcf,epcd->efd/dot_general | solution.py:100
  547.3 107.0 %reduce-scatter.3.cloned.1.call-done = f32[256,1024]{1,0:T(8,128)} async-done(((f32[4096,1024]{1,0:T(8,128)}), f32[256,1024]{1,0:T(8,128)}) %reduce-scatter.3.cloned.1.call-update) | async-done | bytes 1048592 | tf_op jit(solution)/shard_map/reduce_scatter | solution.py:110
  (138 shorter events, 50.1 us)
Async XLA Ops:
  7.2 18.8 %copy-start = (bf16[2,1024,512]{2,1,0:T(8,128)(2,1)S(1)}, bf16[2,1024,512]{2,1,0:T(8,128)(2,1)}, u32[]{:S(2)}) copy-start(bf16[2,1024,512]{2,1,0:T(8,128)(2,1)} %param.37) | copy-start | bytes 6291460
  7.2 47.0 %all-gather.7.cloned.1.call-start = ((), (), s32[]{:S(2)}) async-start(), calls=%async_computation.4 | async-start | bytes 1114112 | tf_op jit(solution)/shard_map/all_gather | solution.py:67
  14.6 116.5 %all-gather.11.cloned.1.call-start = ((), (), s32[]{:S(2)}) async-start(), calls=%async_computation.6 | async-start | bytes 8912896 | tf_op jit(solution)/shard_map/all_gather | solution.py:68
  15.4 337.1 %reduce-scatter.5.cloned.1.call-start = ((), (), s32[]{:S(2)}) async-start(), calls=%async_computation.3 | async-start | bytes 17825792 | tf_op jit(solution)/shard_map/reduce_scatter | solution.py:99
  131.1 6.9 %copy-start.26 = (bf16[2,512,1024]{2,1,0:T(8,128)(2,1)S(1)}, bf16[2,512,1024]{2,1,0:T(8,128)(2,1)}, u32[]{:S(2)}) copy-start(bf16[2,512,1024]{2,1,0:T(8,128)(2,1)} %param.36) | copy-start | bytes 6291460
  138.0 15.7 %copy-start.31 = (bf16[2,16,128,1024]{3,2,0,1:T(8,128)(2,1)}, bf16[2,16,128,1024]{3,2,0,1:T(8,128)(2,1)S(1)}, u32[]{:S(2)}) copy-start(bf16[2,16,128,1024]{3,2,0,1:T(8,128)(2,1)S(1)} %convert_bitcast_fusion) | copy-start | bytes 25165828
  138.0 15.7 %copy-start.25 = (bf16[2,1024,512]{2,1,0:T(8,128)(2,1)S(1)}, bf16[2,1024,512]{2,1,0:T(8,128)(2,1)}, u32[]{:S(2)}) copy-start(bf16[2,1024,512]{2,1,0:T(8,128)(2,1)} %param.35) | copy-start | bytes 6291460
  178.6 252.8 %all-gather.9.cloned.1.call-start = ((), (), s32[]{:S(2)}) async-start(), calls=%async_computation.5 | async-start | bytes 8912896 | tf_op jit(solution)/shard_map/all_gather | solution.py:71
  179.2 5.5 copy-start.28
  180.0 6.6 %copy-start.12 = (bf16[1024,16,64]{0,2,1:T(8,128)(2,1)S(1)}, bf16[1024,16,64]{0,2,1:T(8,128)(2,1)}, u32[]{:S(2)}) copy-start(bf16[1024,16,64]{0,2,1:T(8,128)(2,1)} %param.31) | copy-start | bytes 6291460
  181.9 5.5 copy-start.17
  186.6 3.6 copy-start.21
  189.2 2.8 copy-start.15
  192.0 10.9 %copy-start.9 = (bf16[8,64,2,256]{3,1,2,0:T(8,128)(2,1)}, bf16[8,64,2,256]{3,1,2,0:T(8,128)(2,1)S(1)}, u32[]{:S(2)}) copy-start(bf16[8,64,2,256]{3,1,2,0:T(8,128)(2,1)S(1)} %convolution_convert_fusion.5) | copy-start | bytes 1572868
  198.3 3.0 copy-start.7
  198.3 3.1 copy-start.16
  357.2 297.2 %reduce-scatter.3.cloned.1.call-start = ((), (), s32[]{:S(2)}) async-start(), calls=%async_computation.2 | async-start | bytes 17825792 | tf_op jit(solution)/shard_map/reduce_scatter | solution.py:110
  454.9 13.6 %copy-start.27 = (bf16[2,512,1024]{2,1,0:T(8,128)(2,1)S(1)}, bf16[2,512,1024]{2,1,0:T(8,128)(2,1)}, u32[]{:S(2)}) copy-start(bf16[2,512,1024]{2,1,0:T(8,128)(2,1)} %param.36) | copy-start | bytes 6291460
  513.9 13.4 %copy-start.8 = (bf16[16,64,1024]{2,1,0:T(8,128)(2,1)S(1)}, bf16[16,64,1024]{2,1,0:T(8,128)(2,1)}, u32[]{:S(2)}) copy-start(bf16[16,64,1024]{2,1,0:T(8,128)(2,1)} %param.34) | copy-start | bytes 6291460
  513.9 14.1 %copy-start.3 = (f32[8,256,256,2]{2,1,3,0:T(8,128)S(1)}, f32[8,256,256,2]{2,1,3,0:T(8,128)}, u32[]{:S(2)}) copy-start(f32[8,256,256,2]{2,1,3,0:T(8,128)} %copy-done.2) | copy-start | bytes 12582916
  513.9 14.1 %copy-start.22 = (f32[256,512]{0,1:S(1)}, f32[256,512]{0,1}, u32[]{:S(2)}) copy-start(f32[256,512]{0,1} %copy-done.21) | copy-start | bytes 1572868
  538.5 2.9 copy-start.10
  545.0 111.6 %copy-start.1 = (bf16[2,1024,512]{2,1,0:T(8,128)(2,1)S(1)}, bf16[2,1024,512]{2,1,0:T(8,128)(2,1)}, u32[]{:S(2)}) copy-start(bf16[2,1024,512]{2,1,0:T(8,128)(2,1)} %param.37) | copy-start | bytes 6291460
  545.0 109.4 %copy-start.11 = (bf16[256,1024]{1,0:T(8,128)(2,1)S(1)}, bf16[256,1024]{1,0:T(8,128)(2,1)}, u32[]{:S(2)}) copy-start(bf16[256,1024]{1,0:T(8,128)(2,1)} %get-tuple-element.74) | copy-start | bytes 1572868
  (13 other events, 19.0 us)
Sparse Core Ops, SparseCore 0:
  14.7 39.3 all-gather.6
  56.3 74.7 all-gather.10
  178.7 173.7 reduce-scatter.4
  357.3 74.0 all-gather.8
  480.6 173.7 reduce-scatter.2

commit v2 on v1

v2 whole, which is shorter than its diff:
```python
import functools

import jax
import jax.numpy as jnp
from jax import lax
from jax.experimental import pallas as pl
from jax.experimental.pallas import tpu as pltpu
from jax.sharding import PartitionSpec as P

F32 = jnp.float32
BF16 = jnp.bfloat16
VMEM_BYTES = 66_000_000

NORM_EPS = 1e-6


def rms_norm(values, gain):
    wide = values.astype(jnp.float32)
    scaled = wide * lax.rsqrt(jnp.mean(wide * wide, axis=-1, keepdims=True) + NORM_EPS)
    return (scaled * gain.astype(jnp.float32)).astype(jnp.bfloat16)


def add_rows(first, second):
    return (first.astype(jnp.float32) + second.astype(jnp.float32)).astype(jnp.bfloat16)


def attn_out(x_rows, norm_gain, w_q, w_k, w_v, w_o):
    tokens = x_rows.shape[0]
    heads = w_q.shape[1]
    kv_heads = w_k.shape[1]
    head_dim = w_q.shape[2]
    normed = rms_norm(x_rows, norm_gain)
    query = jnp.einsum('td,dhe->the', normed, w_q, preferred_element_type=jnp.float32).astype(jnp.bfloat16)
    query = query.reshape(tokens, kv_heads, heads // kv_heads, head_dim)
    key_proj = jnp.einsum('td,dge->tge', normed, w_k, preferred_element_type=jnp.float32).astype(jnp.bfloat16)
    val_proj = jnp.einsum('td,dge->tge', normed, w_v, preferred_element_type=jnp.float32).astype(jnp.bfloat16)
    scores = jnp.einsum('tgre,mge->grtm', query, key_proj, preferred_element_type=jnp.float32) * head_dim ** -0.5
    causal = jnp.arange(tokens)[:, None] >= jnp.arange(tokens)[None, :]
    scores = jnp.where(causal, scores, -1e30)
    probs = jax.nn.softmax(scores, axis=-1).astype(jnp.bfloat16)
    context = jnp.einsum('grtm,mge->tgre', probs, val_proj, preferred_element_type=jnp.float32).astype(jnp.bfloat16)
    context = context.reshape(tokens, heads, head_dim)
    return jnp.einsum('the,hed->td', context, w_o, preferred_element_type=jnp.float32).astype(jnp.bfloat16)


def routing_table(expert_ids, slot_ids, gates, experts):
    hit = (expert_ids[:, :, None] == jnp.arange(experts)[None, None, :]) & (slot_ids >= 0)[:, :, None]
    slots = jnp.sum(jnp.where(hit, slot_ids[:, :, None] + 1, 0), axis=1) - 1
    weights = jnp.sum(jnp.where(hit, gates.astype(jnp.float32)[:, :, None], 0.0), axis=1)
    return slots.astype(jnp.bfloat16), weights.astype(jnp.bfloat16)


def mm(left, right):
    return lax.dot_general(left, right, (((1,), (0,)), ((), ())), preferred_element_type=F32)


def mm_nt(left, right):
    return lax.dot_general(left, right, (((1,), (1,)), ((), ())), preferred_element_type=F32)


def mm_tn(left, right):
    return lax.dot_general(left, right, (((0,), (0,)), ((), ())), preferred_element_type=F32)


def exchange_kernel(backward, *refs):
    if backward:
        (rows_ref, u_ref, w1_ref, w3_ref, w2_ref, out_ref, gw1_ref, gw2_ref, gw3_ref,
         got, own, stage, from_core, from_y, from_z, saved, acc1, acc2, acc3,
         own_sem, load_sem, store_sem, g_recv, g_core, g_y, g_z, s_core, r_core, s_y, r_y, s_z, r_z) = refs
    else:
        (rows_ref, w1_ref, w3_ref, w2_ref, out_ref,
         got, own, stage, from_core, from_y, from_z,
         own_sem, g_recv, g_core, g_y, g_z, s_core, r_core, s_y, r_y, s_z, r_z) = refs
    tokens, dim = own.shape[1], own.shape[2]
    half = w1_ref.shape[0]
    me = lax.axis_index('expert')
    z, y, c = lax.div(me, 4), lax.rem(lax.div(me, 2), 2), lax.rem(me, 2)

    def at(zz, yy, cc):
        return (zz * 2 + yy) * 2 + cc

    other_core = at(z, y, 1 - c)
    other_y = at(z, 1 - y, c)

    def z_peer(k):
        return at(lax.rem(z + k, 4), y, c)

    def remote(src, dst, send, recv, peer):
        return pltpu.make_async_remote_copy(src_ref=src, dst_ref=dst, send_sem=send, recv_sem=recv, device_id={'expert': peer}, device_id_type=pl.DeviceIdType.MESH)

    barrier = pltpu.get_barrier_semaphore()
    for peer in (other_core, other_y, z_peer(1), z_peer(2), z_peer(3)):
        pl.semaphore_signal(barrier, inc=1, device_id={'expert': peer}, device_id_type=pl.DeviceIdType.MESH)
    load_own = pltpu.make_async_copy(rows_ref, got.at[me], own_sem)
    load_own.start()
    pl.semaphore_wait(barrier, 5)
    load_own.wait()

    def gather_to_core(slot, block):
        return remote(got.at[block], got.at[block], g_core.at[slot], g_recv.at[block], other_core)

    def gather_to_y(k, block):
        return remote(got.at[block], got.at[block], g_y.at[k], g_recv.at[block], other_y)

    def gather_to_z(k):
        return remote(got.at[me], got.at[me], g_z.at[k - 1], g_recv.at[me], z_peer(k))

    def arrived(block):
        remote(got.at[block], got.at[block], g_core.at[0], g_recv.at[block], other_core).wait_recv()

    gather_to_y(0, me).start()
    for k in (2, 1, 3):
        gather_to_z(k).start()
    gather_to_core(0, me).start()

    def forward_z(k):
        block = at(lax.rem(z + k, 4), y, c)
        arrived(block)
        gather_to_y(k, block).start()
        gather_to_core(k, block).start()

    def order(step):
        i = lax.div(step + 1, 2)
        k = lax.rem(2 * i + lax.rem(lax.div(i, 2), 2), 4)
        across = lax.rem(step + 1, 2) * lax.div(step + 7, 8) + lax.div(step, 7)
        return k, across

    def pair_base(step):
        k, across = order(step)
        return at(lax.rem(z + k, 4), lax.rem(y + across, 2), 0)

    if backward:
        slots = saved.shape[2] // 2

        def load_saved(step):
            start = pl.multiple_of(pair_base(step) * slots, 2 * slots)
            which = lax.rem(step, 2)
            return pltpu.make_async_copy(u_ref.at[:, pl.ds(start, 2 * slots), :], saved.at[which], load_sem.at[which])

        load_saved(0).start()
        acc1[...] = jnp.zeros_like(acc1)
        acc2[...] = jnp.zeros_like(acc2)
        acc3[...] = jnp.zeros_like(acc3)
    else:
        slots = tokens // 2

    sel = (lax.broadcasted_iota(jnp.int32, (16, 16), 1) == me).astype(BF16)
    slot_row = lax.broadcasted_iota(jnp.int32, (slots, tokens), 0).astype(F32)

    def masks(block):
        table = mm(sel, got[block, tokens:, :])
        plain, gated = [], []
        for e in range(half):
            hit = table[0:1, e * tokens:(e + 1) * tokens] == slot_row
            gate = table[0:1, (half + e) * tokens:(half + e + 1) * tokens]
            plain.append(jnp.where(hit, 1.0, 0.0).astype(BF16))
            gated.append(jnp.where(hit, gate, 0.0).astype(BF16))
        return jnp.concatenate(plain, axis=0), jnp.concatenate(gated, axis=0)

    def experts_forward(mine, theirs):
        marks = [masks(block) for block in (mine, theirs)]
        placed = [mm(marks[s][0], got[block, :tokens, :]).astype(BF16) for s, block in enumerate((mine, theirs))]
        outs = []
        for e in range(half):
            rows = jnp.concatenate([part[e * slots:(e + 1) * slots] for part in placed], axis=0)
            act_1 = mm(rows, w1_ref[e]).astype(BF16).astype(F32)
            act_3 = mm(rows, w3_ref[e]).astype(BF16).astype(F32)
            hidden = (act_1 * jax.nn.sigmoid(act_1) * act_3).astype(BF16)
            outs.append(mm(hidden, w2_ref[e]).astype(BF16))

        def combine(s):
            return mm_tn(marks[s][1], jnp.concatenate([out[s * slots:(s + 1) * slots] for out in outs], axis=0))

        return combine

    def experts_backward(mine, theirs, which):
        marks = [masks(block) for block in (mine, theirs)]
        placed = [mm(marks[s][1], got[block, :tokens, :]).astype(BF16) for s, block in enumerate((mine, theirs))]
        outs = []
        for e in range(half):
            rows = saved[which, e]
            d_out = jnp.concatenate([part[e * slots:(e + 1) * slots] for part in placed], axis=0)
            pre_1 = mm(rows, w1_ref[e]).astype(BF16).astype(F32)
            pre_3 = mm(rows, w3_ref[e]).astype(BF16).astype(F32)
            sigma = jax.nn.sigmoid(pre_1)
            silu_1 = pre_1 * sigma
            hidden = (silu_1 * pre_3).astype(BF16)
            acc2[e] += mm_tn(hidden, d_out)
            grad_hid = mm_nt(d_out, w2_ref[e]).astype(BF16).astype(F32)
            grad_a1 = (grad_hid * pre_3 * sigma * (1.0 + pre_1 * (1.0 - sigma))).astype(BF16)
            grad_a3 = (grad_hid * silu_1).astype(BF16)
            acc1[e] += mm_tn(rows, grad_a1)
            acc3[e] += mm_tn(rows, grad_a3)
            outs.append((mm_nt(grad_a1, w1_ref[e]) + mm_nt(grad_a3, w3_ref[e])).astype(BF16))

        def combine(s):
            return mm_tn(marks[s][0], jnp.concatenate([out[s * slots:(s + 1) * slots] for out in outs], axis=0))

        return combine

    def send_core(step):
        which = lax.rem(step, 2)
        return remote(stage.at[which], from_core.at[which], s_core.at[which], r_core.at[which], other_core)

    def send_y(k):
        return remote(own.at[4 + k], from_y.at[k], s_y.at[k], r_y.at[k], other_y)

    def send_z(k):
        return remote(own.at[k], from_z.at[k - 1], s_z.at[k - 1], r_z.at[k - 1], z_peer(k))

    def take_y(k):
        send_y(k).wait_recv()
        own[k] += from_y[k]

    def step_body(step, carry):
        k, across = order(step)
        base = pair_base(step)
        which = lax.rem(step, 2)

        @pl.when(step == 1)
        def _():
            forward_z(2)

        @pl.when(across == 1)
        def _():
            arrived(base + c)
            gather_to_core(4 + k, base + c).start()

        arrived(base + 1 - c)
        if backward:
            @pl.when(step < 7)
            def _():
                load_saved(step + 1).start()
            load_saved(step).wait()
            low, high = base, base + 1
            combine = experts_backward(low, high, which)
        else:
            low, high = base, base + 1
            combine = experts_forward(low, high)

        @pl.when(step >= 2)
        def _():
            send_core(step).wait_send()

        first, second = combine(0), combine(1)

        @pl.when(c == 0)
        def _():
            stage[which] = second
            own[across * 4 + k] = first

        @pl.when(c == 1)
        def _():
            stage[which] = first
            own[across * 4 + k] = second

        send_core(step).start()

        @pl.when(step == 1)
        def _():
            forward_z(1)

        @pl.when(step == 2)
        def _():
            forward_z(3)

        send_core(step).wait_recv()
        own[across * 4 + k] += from_core[which]

        @pl.when(across == 1)
        def _():
            send_y(k).start()

        @pl.when(step == 5)
        def _():
            take_y(2)
            send_z(2).start()

        return carry

    lax.fori_loop(0, 8, step_body, 0)
    if backward:
        stores = [pltpu.make_async_copy(acc, ref, store_sem.at[i]) for i, (acc, ref) in enumerate(((acc1, gw1_ref), (acc2, gw2_ref), (acc3, gw3_ref)))]
        for store in stores:
            store.start()
    for k in (1, 3):
        take_y(k)
        send_z(k).start()
    take_y(0)
    for k in (2, 1, 3):
        send_z(k).wait_recv()
    out_ref[...] = (own[0] + from_z[0] + (from_z[1] + from_z[2])).astype(out_ref.dtype)
    for k in (1, 2, 3):
        send_z(k).wait_send()
        gather_to_z(k).wait_send()
    for k in range(4):
        send_y(k).wait_send()
        gather_to_y(k, me).wait_send()
    for slot in range(8):
        gather_to_core(slot, me).wait_send()
    send_core(0).wait_send()
    send_core(1).wait_send()
    if backward:
        for store in stores:
            store.wait()


def exchange(backward, rows, weights, tokens, saved=None):
    w_1, w_3, w_2 = weights
    dim = rows.shape[1]
    half, ff = w_1.shape[0], w_1.shape[2]
    dma = pltpu.SemaphoreType.DMA
    block = (tokens, dim)
    scratch = [
        pltpu.VMEM((16,) + rows.shape, BF16),
        pltpu.VMEM((8,) + block, F32),
        pltpu.VMEM((2,) + block, F32),
        pltpu.VMEM((2,) + block, F32),
        pltpu.VMEM((4,) + block, F32),
        pltpu.VMEM((3,) + block, F32),
    ]
    tail = [dma((16,)), dma((8,)), dma((4,)), dma((3,)), dma((2,)), dma((2,)), dma((4,)), dma((4,)), dma((3,)), dma((3,))]
    any_spec = pl.BlockSpec(memory_space=pl.ANY)
    vmem_spec = pl.BlockSpec(memory_space=pltpu.VMEM)
    if backward:
        slots = saved.shape[1] // 16
        scratch += [
            pltpu.VMEM((2, half, 2 * slots, dim), BF16),
            pltpu.VMEM((half, dim, ff), F32),
            pltpu.VMEM((half, ff, dim), F32),
            pltpu.VMEM((half, dim, ff), F32),
            dma(()), dma((2,)), dma((3,)),
        ]
        operands = (rows, saved, w_1, w_3, w_2)
        in_specs = [any_spec, any_spec, vmem_spec, vmem_spec, vmem_spec]
        out_shape = [jax.ShapeDtypeStruct(block, BF16), jax.ShapeDtypeStruct((half, dim, ff), F32), jax.ShapeDtypeStruct((half, ff, dim), F32), jax.ShapeDtypeStruct((half, dim, ff), F32)]
        out_specs = [vmem_spec, any_spec, any_spec, any_spec]
    else:
        scratch += [dma(())]
        operands = (rows, w_1, w_3, w_2)
        in_specs = [any_spec, vmem_spec, vmem_spec, vmem_spec]
        out_shape = [jax.ShapeDtypeStruct(block, F32)]
        out_specs = [vmem_spec]
    return pl.pallas_call(
        functools.partial(exchange_kernel, backward),
        out_shape=out_shape,
        in_specs=in_specs,
        out_specs=out_specs,
        scratch_shapes=scratch + tail,
        name='exchange_b' if backward else 'exchange_a',
        compiler_params=pltpu.CompilerParams(collective_id=1 if backward else 0, has_side_effects=True, vmem_limit_bytes=VMEM_BYTES),
    )(*operands)


def device_backward(x_dev, dy_dev, du_dev, norm_1, norm_2, w_q, w_k, w_v, w_o):
    attn_val, attn_pull = jax.vjp(attn_out, x_dev, norm_1, w_q, w_k, w_v, w_o)
    h_dev = add_rows(x_dev, attn_val)
    _, norm_pull = jax.vjp(rms_norm, h_dev, norm_2)
    dh_norm, grad_n2 = norm_pull(du_dev)
    dh_dev = add_rows(dy_dev, dh_norm)
    grad_x, grad_n1, grad_q, grad_k, grad_v, grad_o = attn_pull(dh_dev)
    return (add_rows(dh_dev, grad_x), grad_q.astype(jnp.float32), grad_k.astype(jnp.float32), grad_v.astype(jnp.float32), grad_o.astype(jnp.float32), grad_n1.astype(jnp.float32), grad_n2.astype(jnp.float32))


def solution(mesh):
    group = mesh.shape['expert']

    def local_step(x_a, x_b, dy_b, eid_a, slot_a, gate_a, eid_b, slot_b, gate_b, u_b, norm_1, norm_2, w_q, w_k, w_v, w_o, w_1, w_2, w_3):
        local_experts = w_1.shape[0]
        experts = local_experts * group
        model_dim = x_a.shape[1]

        tokens = x_a.shape[0]

        def with_routing(rows, expert_ids, slot_ids, gates):
            slots, weights = routing_table(expert_ids, slot_ids, gates, experts)
            table = jnp.stack([slots, weights], axis=1).reshape(tokens, 2, group, local_experts)
            table = table.transpose(2, 1, 3, 0).reshape(group, 2 * local_experts * tokens)
            table = jnp.pad(table, ((0, 0), (0, model_dim - table.shape[1])))
            return jnp.concatenate([rows, table], axis=0)

        weights = (w_1, w_3, w_2)
        du_rows, grad_w1, grad_w2, grad_w3 = exchange(True, with_routing(dy_b, eid_b, slot_b, gate_b), weights, tokens, u_b)
        h_a = add_rows(x_a, attn_out(x_a, norm_1, w_q, w_k, w_v, w_o))
        u_a = rms_norm(h_a, norm_2)
        mixed = exchange(False, with_routing(u_a, eid_a, slot_a, gate_a), weights, tokens)[0]
        y_a = (h_a.astype(jnp.float32) + mixed).astype(jnp.bfloat16)
        dx_b, g_q, g_k, g_v, g_o, g_n1, g_n2 = device_backward(x_b, dy_b, du_rows, norm_1, norm_2, w_q, w_k, w_v, w_o)
        return (y_a, dx_b, grad_w1, grad_w2, grad_w3, g_q[None], g_k[None], g_v[None], g_o[None], g_n1[None], g_n2[None])

    row_spec = P(('data', 'expert'), None)
    cube_spec = P(('data', 'expert'), None, None)
    quad_spec = P(('data', 'expert'), None, None, None)
    expert_spec = P('expert', None, None)
    in_specs = (row_spec, row_spec, row_spec, row_spec, row_spec, row_spec, row_spec, row_spec, row_spec, cube_spec, P(), P(), P(), P(), P(), P(), expert_spec, expert_spec, expert_spec)
    out_specs = (row_spec, row_spec, cube_spec, cube_spec, cube_spec, quad_spec, quad_spec, quad_spec, quad_spec, row_spec, row_spec)
    return jax.shard_map(local_step, mesh=mesh, in_specs=in_specs, out_specs=out_specs, check_vma=False)
```

time: 668 us -> 459 us (0.69)
  the two profiles are of different devices: /device:TPU:0 before, /device:TPU:22 now
where the time goes in v2:
time: 459 us
  Pallas kernels  387 us (84%)
  matrix products  32.9 us (7%)
  other arithmetic  25.5 us (6%)
  local copies, waits for them, and re-layouts  11.9 us (3%)
    pallas_call x2, Pallas kernels, exchange(): pl.pallas_call(functools.partial(exchange_kernel, backward), out_shape=ou...  387 us
    unnamed x75, local copies, waits for them, and re-layouts  11.8 us
    unnamed x9, matrix products  10.9 us

profile of v2, /device:TPU:22, one launch (start us, length us, event | category | flops | bytes accessed | tf_op | source)
XLA Modules:
  0.0 458.5 jit_solution(14757945085085842407)
XLA Ops:
  4.6 1.2 fusion.46
  6.5 2.6 bitcast_convert_fusion.5
  15.3 1.5 fusion.44
  18.1 192.6 %exchange_b.1 = (bf16[256,1024]{1,0:T(8,128)(2,1)}, f32[2,1024,512]{2,1,0:T(8,128)}, f32[2,512,1024]{2,1,0:T(8,128)}, f32[2,1024,512]{2,1,0:T(8,128)}) custom-call(bf16[272,1024]{1,0:T(8,128)(2,1)} %pad_maximum_fusion.1.refs_0_, bf16[2,2048,1024]{2,1,0:T(8,128)(2,1)} %refs_1_.3, bf16[2,1024,512]{2,1,0:T(8,128)(2,1)} %refs_2_.3, ...), custom_call_target="tpu_custom_call" | custom-call | tf_op jit(solution)/shard_map/exchange_b/pallas_call | solution.py:344
  210.7 1.8 fusion.33
  213.7 3.4 bitcast_convert_fusion.4
  217.1 1.4 fusion.84
  218.5 4.7 %fusion.102 = (f32[8,2,256]{2,1,0:T(2,128)S(1)}, f32[8,2,256,256]{2,3,1,0:T(8,128)}) fusion(pred[256,256]{0,1:T(8,128)(4,1)S(1)} %iota_compare_fusion.3, bf16[256,8,2,64]{0,3,2,1:T(8,128)(2,1)} %bitcast.266, f32[256,8,64]{0,2,1:T(8,128)} %bitcast.267), kind=kOutput, calls=%fused_computation.159 | convolution fusion | flops 138543360 | bytes 5324800 | tf_op jit(solution)/shard_map/sub | solution.py:40
  223.8 2.9 fusion.15
  227.6 1.2 add_convert_fusion.1
  229.7 194.4 %exchange_a.1 = f32[256,1024]{1,0:T(8,128)} custom-call(bf16[272,1024]{1,0:T(8,128)(2,1)} %pad_maximum_fusion.refs_0_, bf16[2,1024,512]{2,1,0:T(8,128)(2,1)} %refs_2_.3, bf16[2,1024,512]{2,1,0:T(8,128)(2,1)} %refs_3_.3, bf16[2,512,1024]{2,1,0:T(8,128)(2,1)} %refs_4_.1), custom_call_target="tpu_custom_call" | custom-call | tf_op jit(solution)/shard_map/exchange_a/pallas_call | solution.py:344
  424.1 2.5 fusion.41
  426.6 2.5 convolution_convert_fusion.2
  429.1 1.5 fusion.7
  430.7 1.7 fusion.5
  438.9 2.3 bitcast_convert_fusion.1
  441.7 1.5 bitcast_convert_fusion.3
  443.7 1.5 bitcast_convert_fusion.2
  445.2 2.7 bitcast_convert_fusion
  449.1 2.1 copy.60
  451.2 1.6 copy-done.13
  452.8 2.1 copy.61
  454.9 1.6 copy-done.12
  456.5 2.0 copy.62
  (124 shorter events, 24.0 us)
Async XLA Ops:
  0.6 8.5 %copy-start.4 = (bf16[256,1024]{1,0:T(8,128)(2,1)S(1)}, bf16[256,1024]{1,0:T(8,128)(2,1)}, u32[]{:S(2)}) copy-start(bf16[256,1024]{1,0:T(8,128)(2,1)} %param.20) | copy-start | bytes 1572868
  0.7 8.5 %copy-start.33 = (bf16[1024,8,64]{0,2,1:T(8,128)(2,1)S(1)}, bf16[1024,8,64]{0,2,1:T(8,128)(2,1)}, u32[]{:S(2)}) copy-start(bf16[1024,8,64]{0,2,1:T(8,128)(2,1)} %param.32) | copy-start | bytes 3145732
  12.7 4.2 copy-start.2
  12.7 2.6 copy-start.5
  13.4 3.5 copy-start.28
  13.4 3.5 copy-start.27
  13.4 3.5 copy-start.26
  13.4 3.8 copy-start.15
  13.9 2.9 copy-start.24
  14.4 2.4 copy-start.9
  18.1 192.6 %copy-start.29 = (bf16[1024]{0:T(1024)(128)(2,1)S(1)}, bf16[1024]{0:T(1024)(128)(2,1)}, u32[]{:S(2)}) copy-start(bf16[1024]{0:T(1024)(128)(2,1)} %param.30) | copy-start | bytes 6148
  210.6 6.5 %copy-start.19 = (bf16[256,1024]{1,0:T(8,128)(2,1)S(1)}, bf16[256,1024]{1,0:T(8,128)(2,1)}, u32[]{:S(2)}) copy-start(bf16[256,1024]{1,0:T(8,128)(2,1)} %param.19) | copy-start | bytes 1572868
  210.6 6.5 %copy-start.34 = (bf16[1024,8,64]{0,2,1:T(8,128)(2,1)S(1)}, bf16[1024,8,64]{0,2,1:T(8,128)(2,1)}, u32[]{:S(2)}) copy-start(bf16[1024,8,64]{0,2,1:T(8,128)(2,1)} %param.32) | copy-start | bytes 3145732
  218.5 4.7 %copy-start.31 = (bf16[1024,8,64]{0,2,1:T(8,128)(2,1)S(1)}, bf16[1024,8,64]{0,2,1:T(8,128)(2,1)}, u32[]{:S(2)}) copy-start(bf16[1024,8,64]{0,2,1:T(8,128)(2,1)} %param.33) | copy-start | bytes 3145732
  223.8 2.9 copy-start.6
  223.8 3.8 copy-start.8
  223.8 3.8 copy-start.16
  223.8 3.8 copy-start.17
  424.1 5.0 %copy-start.1 = (f32[8,256,256,2]{2,1,3,0:T(8,128)S(1)}, f32[8,256,256,2]{2,1,3,0:T(8,128)}, u32[]{:S(2)}) copy-start(f32[8,256,256,2]{2,1,3,0:T(8,128)} %copy-done) | copy-start | bytes 12582916
  424.1 5.0 %copy-start.25 = (f32[256,512]{0,1:S(1)}, f32[256,512]{0,1}, u32[]{:S(2)}) copy-start(f32[256,512]{0,1} %copy-done.24) | copy-start | bytes 1572868
  432.4 2.4 copy-start.32
  443.7 5.4 %copy-start.14 = (f32[2,1024,512]{2,1,0:T(8,128)S(1)}, f32[2,1024,512]{2,1,0:T(8,128)}, u32[]{:S(2)}) copy-start(f32[2,1024,512]{2,1,0:T(8,128)} %get-tuple-element.51) | copy-start | bytes 12582916
  449.1 3.7 copy-start.13
  452.8 3.7 copy-start.12
  (12 other events, 20.4 us)

commit v3 on v2

--- a/solution.py
+++ b/solution.py
@@ -82,52 +82,75 @@
     other_core = at(z, y, 1 - c)
     other_y = at(z, 1 - y, c)
 
-    def z_peer(k):
-        return at(lax.rem(z + k, 4), y, c)
+    upper, odd = lax.div(z, 2), lax.rem(z, 2)
+    at_end = jnp.logical_or(z == 0, z == 3)
+    inside = jnp.logical_and(z > 0, z < 3)
+
+    def column(n):
+        far = lax.div(n, 2)
+        return far * (n + upper * (3 - 2 * n)) + (1 - far) * (2 * upper + lax.rem(odd + n, 2))
+
+    right, left = at(lax.rem(z + 1, 4), y, c), at(lax.rem(z + 3, 4), y, c)
 
     def remote(src, dst, send, recv, peer):
         return pltpu.make_async_remote_copy(src_ref=src, dst_ref=dst, send_sem=send, recv_sem=recv, device_id={'expert': peer}, device_id_type=pl.DeviceIdType.MESH)
 
     barrier = pltpu.get_barrier_semaphore()
-    for peer in (other_core, other_y, z_peer(1), z_peer(2), z_peer(3)):
+    for peer in (other_core, other_y, right, left):
         pl.semaphore_signal(barrier, inc=1, device_id={'expert': peer}, device_id_type=pl.DeviceIdType.MESH)
     load_own = pltpu.make_async_copy(rows_ref, got.at[me], own_sem)
     load_own.start()
-    pl.semaphore_wait(barrier, 5)
+    pl.semaphore_wait(barrier, 4)
     load_own.wait()
 
     def gather_to_core(slot, block):
         return remote(got.at[block], got.at[block], g_core.at[slot], g_recv.at[block], other_core)
 
-    def gather_to_y(k, block):
-        return remote(got.at[block], got.at[block], g_y.at[k], g_recv.at[block], other_y)
-
-    def gather_to_z(k):
-        return remote(got.at[me], got.at[me], g_z.at[k - 1], g_recv.at[me], z_peer(k))
+    def gather_to_y(n, block):
+        return remote(got.at[block], got.at[block], g_y.at[n], g_recv.at[block], other_y)
+
+    def gather_along(sem, block, peer):
+        return remote(got.at[block], got.at[block], g_z.at[sem], g_recv.at[block], peer)
 
     def arrived(block):
         remote(got.at[block], got.at[block], g_core.at[0], g_recv.at[block], other_core).wait_recv()
 
+    def along_z(n, action):
+        source = column(n)
+        block = at(source, y, c)
+
+        @pl.when(jnp.logical_and(source <= z, z < 3))
+        def _():
+            action(gather_along(n, block, right))
+
+        @pl.when(jnp.logical_and(source >= z, z > 0))
+        def _():
+            action(gather_along(n if n else 4, block, left))
+
+    def start(copy):
+        copy.start()
+
+    def sent(copy):
+        copy.wait_send()
+
+    along_z(0, start)
     gather_to_y(0, me).start()
-    for k in (2, 1, 3):
-        gather_to_z(k).start()
     gather_to_core(0, me).start()
 
-    def forward_z(k):
-        block = at(lax.rem(z + k, 4), y, c)
+    def pass_on(n):
+        block = at(column(n), y, c)
         arrived(block)
-        gather_to_y(k, block).start()
-        gather_to_core(k, block).start()
+        along_z(n, start)
+        gather_to_y(n, block).start()
+        gather_to_core(n, block).start()
 
     def order(step):
-        i = lax.div(step + 1, 2)
-        k = lax.rem(2 * i + lax.rem(lax.div(i, 2), 2), 4)
-        across = lax.rem(step + 1, 2) * lax.div(step + 7, 8) + lax.div(step, 7)
-        return k, across
+        late = lax.div(step, 4)
+        return step + late * (7 - 2 * step), late
 
     def pair_base(step):
-        k, across = order(step)
-        return at(lax.rem(z + k, 4), lax.rem(y + across, 2), 0)
+        n, across = order(step)
+        return at(column(n), lax.rem(y + across, 2), 0)
 
     if backward:
         slots = saved.shape[2] // 2
@@ -202,29 +225,54 @@
         which = lax.rem(step, 2)
         return remote(stage.at[which], from_core.at[which], s_core.at[which], r_core.at[which], other_core)
 
-    def send_y(k):
-        return remote(own.at[4 + k], from_y.at[k], s_y.at[k], r_y.at[k], other_y)
-
-    def send_z(k):
-        return remote(own.at[k], from_z.at[k - 1], s_z.at[k - 1], r_z.at[k - 1], z_peer(k))
-
-    def take_y(k):
-        send_y(k).wait_recv()
-        own[k] += from_y[k]
+    def send_y(n):
+        return remote(own.at[4 + n], from_y.at[n], s_y.at[n], r_y.at[n], other_y)
+
+    def take_y(n):
+        send_y(n).wait_recv()
+        own[n] += from_y[n]
+
+    def chain(n, action):
+        goal = column(n)
+
+        @pl.when(goal > z)
+        def _():
+            action(remote(own.at[n], from_z.at[goal], s_z.at[n - 1], r_z.at[goal], right))
+
+        @pl.when(goal == z - 1)
+        def _():
+            action(remote(own.at[n], from_z.at[4], s_z.at[n - 1], r_z.at[4], left))
+
+        @pl.when(goal < z - 1)
+        def _():
+            action(remote(own.at[n], from_z.at[goal], s_z.at[n - 1], r_z.at[goal], left))
+
+    def take_z(n, slot):
+        remote(own.at[n], from_z.at[slot], s_z.at[0], r_z.at[slot], left).wait_recv()
+        own[n] += from_z[slot]
 
     def step_body(step, carry):
-        k, across = order(step)
+        n, across = order(step)
         base = pair_base(step)
         which = lax.rem(step, 2)
 
         @pl.when(step == 1)
         def _():
-            forward_z(2)
-
-        @pl.when(across == 1)
-        def _():
-            arrived(base + c)
-            gather_to_core(4 + k, base + c).start()
+            pass_on(1)
+
+        @pl.when(jnp.logical_or(jnp.logical_and(step == 1, inside), jnp.logical_and(step == 2, at_end)))
+        def _():
+            pass_on(2)
+
+        @pl.when(jnp.logical_or(jnp.logical_and(step == 2, inside), jnp.logical_and(step == 3, at_end)))
+        def _():
+            pass_on(3)
+
+        @pl.when(jnp.logical_and(step >= 1, step <= 4))
+        def _():
+            block = at(column(step - 1), 1 - y, c)
+            arrived(block)
+            gather_to_core(3 + step, block).start()
 
         arrived(base + 1 - c)
         if backward:
@@ -247,34 +295,29 @@
         @pl.when(c == 0)
         def _():
             stage[which] = second
-            own[across * 4 + k] = first
+            own[across * 4 + n] = first
 
         @pl.when(c == 1)
         def _():
             stage[which] = first
-            own[across * 4 + k] = second
+            own[across * 4 + n] = second
 
         send_core(step).start()
 
-        @pl.when(step == 1)
-        def _():
-            forward_z(1)
-
-        @pl.when(step == 2)
-        def _():
-            forward_z(3)
-
         send_core(step).wait_recv()
-        own[across * 4 + k] += from_core[which]
+        own[across * 4 + n] += from_core[which]
 
         @pl.when(across == 1)
         def _():
-            send_y(k).start()
-
-        @pl.when(step == 5)
-        def _():
-            take_y(2)
-            send_z(2).start()
+            send_y(n).start()
+
+        @pl.when(step == 6)
+        def _():
+            take_y(3)
+
+            @pl.when(at_end)
+            def _():
+                chain(3, start)
 
         return carry
 
@@ -283,19 +326,39 @@
         stores = [pltpu.make_async_copy(acc, ref, store_sem.at[i]) for i, (acc, ref) in enumerate(((acc1, gw1_ref), (acc2, gw2_ref), (acc3, gw3_ref)))]
         for store in stores:
             store.start()
-    for k in (1, 3):
-        take_y(k)
-        send_z(k).start()
+
+    def join(n):
+        @pl.when(inside)
+        def _():
+            take_z(n, column(n))
+            chain(n, start)
+
+    join(3)
+    for n in (2, 1):
+        take_y(n)
+
+        @pl.when(at_end)
+        def _():
+            chain(n, start)
+
+        join(n)
     take_y(0)
-    for k in (2, 1, 3):
-        send_z(k).wait_recv()
-    out_ref[...] = (own[0] + from_z[0] + (from_z[1] + from_z[2])).astype(out_ref.dtype)
-    for k in (1, 2, 3):
-        send_z(k).wait_send()
-        gather_to_z(k).wait_send()
-    for k in range(4):
-        send_y(k).wait_send()
-        gather_to_y(k, me).wait_send()
+
+    @pl.when(z > 0)
+    def _():
+        take_z(0, z)
+
+    @pl.when(z < 3)
+    def _():
+        take_z(0, 4)
+
+    out_ref[...] = own[0].astype(out_ref.dtype)
+    for n in (3, 2, 1):
+        chain(n, sent)
+    for n in range(4):
+        along_z(n, sent)
+        send_y(n).wait_send()
+        gather_to_y(n, me).wait_send()
     for slot in range(8):
         gather_to_core(slot, me).wait_send()
     send_core(0).wait_send()
@@ -317,9 +380,9 @@
         pltpu.VMEM((2,) + block, F32),
         pltpu.VMEM((2,) + block, F32),
         pltpu.VMEM((4,) + block, F32),
-        pltpu.VMEM((3,) + block, F32),
+        pltpu.VMEM((5,) + block, F32),
     ]
-    tail = [dma((16,)), dma((8,)), dma((4,)), dma((3,)), dma((2,)), dma((2,)), dma((4,)), dma((4,)), dma((3,)), dma((3,))]
+    tail = [dma((16,)), dma((8,)), dma((4,)), dma((5,)), dma((2,)), dma((2,)), dma((4,)), dma((4,)), dma((3,)), dma((5,))]
     any_spec = pl.BlockSpec(memory_space=pl.ANY)
     vmem_spec = pl.BlockSpec(memory_space=pltpu.VMEM)
     if backward:

time: 459 us -> 387 us (0.84)
  the two profiles are of different devices: /device:TPU:22 before, /device:TPU:0 now
where the time goes in v3:
time: 387 us; the launch traced here: 386 us
  Pallas kernels  315 us (81%)
  matrix products  32.9 us (9%)
  other arithmetic  25.5 us (7%)
  local copies, waits for them, and re-layouts  11.9 us (3%)
    pallas_call x2, Pallas kernels, exchange(): pl.pallas_call(functools.partial(exchange_kernel, backward), out_shape=ou...  315 us
    unnamed x75, local copies, waits for them, and re-layouts  11.8 us
    unnamed x9, matrix products  10.9 us

profile of v3, /device:TPU:0, one launch (start us, length us, event | category | flops | bytes accessed | tf_op | source)
XLA Modules:
  0.0 386.2 jit_solution(2430659644980393778)
XLA Ops:
  4.6 1.2 fusion.46
  6.5 2.6 bitcast_convert_fusion.5
  15.3 1.5 fusion.44
  18.1 161.6 %exchange_b.1 = (bf16[256,1024]{1,0:T(8,128)(2,1)}, f32[2,1024,512]{2,1,0:T(8,128)}, f32[2,512,1024]{2,1,0:T(8,128)}, f32[2,1024,512]{2,1,0:T(8,128)}) custom-call(bf16[272,1024]{1,0:T(8,128)(2,1)} %pad_maximum_fusion.1.refs_0_, bf16[2,2048,1024]{2,1,0:T(8,128)(2,1)} %refs_1_.3, bf16[2,1024,512]{2,1,0:T(8,128)(2,1)} %refs_2_.3, ...), custom_call_target="tpu_custom_call" | custom-call | tf_op jit(solution)/shard_map/exchange_b/pallas_call | solution.py:407
  179.7 1.8 fusion.33
  182.7 3.4 bitcast_convert_fusion.4
  186.1 1.4 fusion.84
  187.5 4.7 %fusion.102 = (f32[8,2,256]{2,1,0:T(2,128)S(1)}, f32[8,2,256,256]{2,3,1,0:T(8,128)}) fusion(pred[256,256]{0,1:T(8,128)(4,1)S(1)} %iota_compare_fusion.3, bf16[256,8,2,64]{0,3,2,1:T(8,128)(2,1)} %bitcast.266, f32[256,8,64]{0,2,1:T(8,128)} %bitcast.267), kind=kOutput, calls=%fused_computation.159 | convolution fusion | flops 138543360 | bytes 5324800 | tf_op jit(solution)/shard_map/sub | solution.py:40
  192.9 2.9 fusion.15
  196.6 1.2 add_convert_fusion.1
  198.7 153.0 %exchange_a.1 = f32[256,1024]{1,0:T(8,128)} custom-call(bf16[272,1024]{1,0:T(8,128)(2,1)} %pad_maximum_fusion.refs_0_, bf16[2,1024,512]{2,1,0:T(8,128)(2,1)} %refs_2_.3, bf16[2,1024,512]{2,1,0:T(8,128)(2,1)} %refs_3_.3, bf16[2,512,1024]{2,1,0:T(8,128)(2,1)} %refs_4_.1), custom_call_target="tpu_custom_call" | custom-call | tf_op jit(solution)/shard_map/exchange_a/pallas_call | solution.py:407
  351.8 2.5 fusion.41
  354.3 2.5 convolution_convert_fusion.2
  356.8 1.5 fusion.7
  358.4 1.7 fusion.5
  366.5 2.3 bitcast_convert_fusion.1
  369.4 1.5 bitcast_convert_fusion.3
  371.4 1.5 bitcast_convert_fusion.2
  372.8 2.7 bitcast_convert_fusion
  376.8 2.1 copy.60
  378.9 1.6 copy-done.13
  380.5 2.1 copy.61
  382.6 1.6 copy-done.12
  384.2 2.0 copy.62
  (124 shorter events, 24.0 us)
Async XLA Ops:
  0.6 8.5 %copy-start.4 = (bf16[256,1024]{1,0:T(8,128)(2,1)S(1)}, bf16[256,1024]{1,0:T(8,128)(2,1)}, u32[]{:S(2)}) copy-start(bf16[256,1024]{1,0:T(8,128)(2,1)} %param.20) | copy-start | bytes 1572868
  0.7 8.5 %copy-start.33 = (bf16[1024,8,64]{0,2,1:T(8,128)(2,1)S(1)}, bf16[1024,8,64]{0,2,1:T(8,128)(2,1)}, u32[]{:S(2)}) copy-start(bf16[1024,8,64]{0,2,1:T(8,128)(2,1)} %param.32) | copy-start | bytes 3145732
  12.7 4.2 %copy-start.2 = (bf16[8,2,256,256]{2,3,1,0:T(8,128)(2,1)}, bf16[8,2,256,256]{2,3,1,0:T(8,128)(2,1)S(1)}, u32[]{:S(2)}) copy-start(bf16[8,2,256,256]{2,3,1,0:T(8,128)(2,1)S(1)} %divide_convert_fusion) | copy-start | bytes 6291460
  12.7 2.6 copy-start.5
  13.4 3.5 copy-start.28
  13.4 3.5 copy-start.27
  13.4 3.5 copy-start.26
  13.4 3.8 copy-start.15
  14.0 2.9 copy-start.24
  14.4 2.4 copy-start.9
  18.1 161.6 %copy-start.29 = (bf16[1024]{0:T(1024)(128)(2,1)S(1)}, bf16[1024]{0:T(1024)(128)(2,1)}, u32[]{:S(2)}) copy-start(bf16[1024]{0:T(1024)(128)(2,1)} %param.30) | copy-start | bytes 6148
  179.6 6.5 %copy-start.19 = (bf16[256,1024]{1,0:T(8,128)(2,1)S(1)}, bf16[256,1024]{1,0:T(8,128)(2,1)}, u32[]{:S(2)}) copy-start(bf16[256,1024]{1,0:T(8,128)(2,1)} %param.19) | copy-start | bytes 1572868
  179.7 6.5 %copy-start.34 = (bf16[1024,8,64]{0,2,1:T(8,128)(2,1)S(1)}, bf16[1024,8,64]{0,2,1:T(8,128)(2,1)}, u32[]{:S(2)}) copy-start(bf16[1024,8,64]{0,2,1:T(8,128)(2,1)} %param.32) | copy-start | bytes 3145732
  187.5 4.8 %copy-start.31 = (bf16[1024,8,64]{0,2,1:T(8,128)(2,1)S(1)}, bf16[1024,8,64]{0,2,1:T(8,128)(2,1)}, u32[]{:S(2)}) copy-start(bf16[1024,8,64]{0,2,1:T(8,128)(2,1)} %param.33) | copy-start | bytes 3145732
  192.8 2.9 copy-start.6
  192.8 3.8 copy-start.8
  192.8 3.8 copy-start.16
  192.9 3.8 copy-start.17
  351.8 5.0 %copy-start.1 = (f32[8,256,256,2]{2,1,3,0:T(8,128)S(1)}, f32[8,256,256,2]{2,1,3,0:T(8,128)}, u32[]{:S(2)}) copy-start(f32[8,256,256,2]{2,1,3,0:T(8,128)} %copy-done) | copy-start | bytes 12582916
  351.8 5.0 %copy-start.25 = (f32[256,512]{0,1:S(1)}, f32[256,512]{0,1}, u32[]{:S(2)}) copy-start(f32[256,512]{0,1} %copy-done.24) | copy-start | bytes 1572868
  360.1 2.4 copy-start.32
  371.4 5.4 %copy-start.14 = (f32[2,1024,512]{2,1,0:T(8,128)S(1)}, f32[2,1024,512]{2,1,0:T(8,128)}, u32[]{:S(2)}) copy-start(f32[2,1024,512]{2,1,0:T(8,128)} %get-tuple-element.51) | copy-start | bytes 12582916
  376.8 3.7 copy-start.13
  380.5 3.7 copy-start.12
  (12 other events, 20.4 us)

commit v4 on v3

--- a/solution.py
+++ b/solution.py
@@ -14,35 +14,6 @@
 NORM_EPS = 1e-6
 
 
-def rms_norm(values, gain):
-    wide = values.astype(jnp.float32)
-    scaled = wide * lax.rsqrt(jnp.mean(wide * wide, axis=-1, keepdims=True) + NORM_EPS)
-    return (scaled * gain.astype(jnp.float32)).astype(jnp.bfloat16)
-
-
-def add_rows(first, second):
-    return (first.astype(jnp.float32) + second.astype(jnp.float32)).astype(jnp.bfloat16)
-
-
-def attn_out(x_rows, norm_gain, w_q, w_k, w_v, w_o):
-    tokens = x_rows.shape[0]
-    heads = w_q.shape[1]
-    kv_heads = w_k.shape[1]
-    head_dim = w_q.shape[2]
-    normed = rms_norm(x_rows, norm_gain)
-    query = jnp.einsum('td,dhe->the', normed, w_q, preferred_element_type=jnp.float32).astype(jnp.bfloat16)
-    query = query.reshape(tokens, kv_heads, heads // kv_heads, head_dim)
-    key_proj = jnp.einsum('td,dge->tge', normed, w_k, preferred_element_type=jnp.float32).astype(jnp.bfloat16)
-    val_proj = jnp.einsum('td,dge->tge', normed, w_v, preferred_element_type=jnp.float32).astype(jnp.bfloat16)
-    scores = jnp.einsum('tgre,mge->grtm', query, key_proj, preferred_element_type=jnp.float32) * head_dim ** -0.5
-    causal = jnp.arange(tokens)[:, None] >= jnp.arange(tokens)[None, :]
-    scores = jnp.where(causal, scores, -1e30)
-    probs = jax.nn.softmax(scores, axis=-1).astype(jnp.bfloat16)
-    context = jnp.einsum('grtm,mge->tgre', probs, val_proj, preferred_element_type=jnp.float32).astype(jnp.bfloat16)
-    context = context.reshape(tokens, heads, head_dim)
-    return jnp.einsum('the,hed->td', context, w_o, preferred_element_type=jnp.float32).astype(jnp.bfloat16)
-
-
 def routing_table(expert_ids, slot_ids, gates, experts):
     hit = (expert_ids[:, :, None] == jnp.arange(experts)[None, None, :]) & (slot_ids >= 0)[:, :, None]
     slots = jnp.sum(jnp.where(hit, slot_ids[:, :, None] + 1, 0), axis=1) - 1
@@ -62,14 +33,121 @@
     return lax.dot_general(left, right, (((0,), (0,)), ((), ())), preferred_element_type=F32)
 
 
-def exchange_kernel(backward, *refs):
-    if backward:
-        (rows_ref, u_ref, w1_ref, w3_ref, w2_ref, out_ref, gw1_ref, gw2_ref, gw3_ref,
-         got, own, stage, from_core, from_y, from_z, saved, acc1, acc2, acc3,
+class Attention:
+    def __init__(self, got, proj, ctx, x_ref, n1_ref, n2_ref, head_dim):
+        self.got, self.proj, self.ctx, self.x_ref, self.n1_ref, self.n2_ref = got, proj, ctx, x_ref, n1_ref, n2_ref
+        self.tokens, self.dim = x_ref.shape
+        self.head_dim = head_dim
+        self.kv = self.dim // 2
+        self.chunk = self.dim // 4
+        self.low = lax.broadcasted_iota(jnp.int32, (self.tokens, 2 * head_dim), 1) < head_dim
+        row = lax.broadcasted_iota(jnp.int32, (2 * self.tokens, self.tokens), 0)
+        row = jnp.where(row >= self.tokens, row - self.tokens, row)
+        self.causal = row >= lax.broadcasted_iota(jnp.int32, (2 * self.tokens, self.tokens), 1)
+
+    def copies(self, wq, wk, wv, wo, sems):
+        n, out = self.chunk, []
+        for i in range(4):
+            rows = pl.ds(i * n, n)
+            out.append(pltpu.make_async_copy(wq.at[rows], self.got.at[i, pl.ds(0, n)], sems.at[i]))
+            out.append(pltpu.make_async_copy(wo.at[rows], self.got.at[4 + i, pl.ds(0, n)], sems.at[4 + i]))
+            out.append(pltpu.make_async_copy(wk.at[rows], self.got.at[8 + i, pl.ds(0, n), pl.ds(0, self.kv)], sems.at[8 + i]))
+            out.append(pltpu.make_async_copy(wv.at[rows], self.got.at[8 + i, pl.ds(0, n), pl.ds(self.kv, self.kv)], sems.at[12 + i]))
+        return out
+
+    def weight(self, i):
+        return self.got[i, :self.chunk, :]
+
+    def scale(self, wide):
+        return lax.rsqrt(jnp.mean(wide * wide, axis=-1, keepdims=True) + NORM_EPS)
+
+    def norm(self, wide, gain_ref):
+        return (wide * self.scale(wide) * gain_ref[...].astype(F32)).astype(BF16)
+
+    def norm_pull(self, wide, gain_ref, grad):
+        inv = self.scale(wide)
+        gain_grad = jnp.sum(grad * (wide * inv), axis=0, keepdims=True).astype(BF16).astype(F32)
+        inner = grad * gain_ref[...].astype(F32)
+        row_grad = inv * inner - wide * (inv * inv * inv * jnp.mean(inner * wide, axis=-1, keepdims=True))
+        return row_grad.astype(BF16), gain_grad
+
+    def normed(self):
+        return self.norm(self.x_ref[...].astype(F32), self.n1_ref)
+
+    def part(self, rows, i):
+        return rows[:, i * self.chunk:(i + 1) * self.chunk]
+
+    def project(self):
+        rows = self.normed()
+        self.proj[:, :self.dim] = sum(mm(self.part(rows, i), self.weight(i)) for i in range(4)).astype(BF16)
+        self.proj[:, self.dim:] = sum(mm(self.part(rows, i), self.weight(8 + i)) for i in range(4)).astype(BF16)
+
+    def stacked(self, ref, start):
+        pair = ref[:, pl.ds(start, 2 * self.head_dim)].astype(F32)
+        return jnp.concatenate([jnp.where(self.low, pair, 0.0), jnp.where(self.low, 0.0, pair)], axis=0).astype(BF16)
+
+    def doubled(self, start, odd):
+        pair = self.proj[:, pl.ds(start, 2 * self.head_dim)].astype(F32)
+        turned = pltpu.roll(pair, self.head_dim, 1)
+        return (jnp.where(self.low, turned, pair) if odd else jnp.where(self.low, pair, turned)).astype(BF16)
+
+    def merged(self, both):
+        return jnp.where(self.low, both[:self.tokens], both[self.tokens:])
+
+    def group(self, quad, odd):
+        width = 2 * self.head_dim
+        at = pl.multiple_of((2 * quad + odd) * width, width)
+        kv_at = pl.multiple_of(quad * width, width)
+        query = self.stacked(self.proj, at)
+        keys = self.doubled(self.dim + kv_at, odd)
+        vals = self.doubled(self.dim + self.kv + kv_at, odd)
+        scores = jnp.where(self.causal, mm_nt(query, keys) * self.head_dim ** -0.5, -1e30)
+        powers = jnp.exp(scores - jnp.max(scores, axis=-1, keepdims=True))
+        return at, kv_at, query, keys, vals, powers / jnp.sum(powers, axis=-1, keepdims=True)
+
+    def heads(self):
+        def body(quad, carry):
+            for odd in range(2):
+                at, _, _, _, vals, probs = self.group(quad, odd)
+                self.ctx[:, pl.ds(at, 2 * self.head_dim)] = self.merged(mm(probs.astype(BF16), vals)).astype(BF16)
+            return carry
+
+        lax.fori_loop(0, self.kv // (2 * self.head_dim), body, 0)
+
+    def hidden(self):
+        attn = sum(mm(self.part(self.ctx[...], i), self.weight(4 + i)) for i in range(4)).astype(BF16)
+        return (self.x_ref[...].astype(F32) + attn.astype(F32)).astype(BF16)
+
+    def pull_heads(self, d_ctx, d_proj):
+        def fold(both):
+            return both + pltpu.roll(both, self.head_dim, 1)
+
+        def body(quad, carry):
+            d_keys, d_vals = [], []
+            for odd in range(2):
+                at, kv_at, query, keys, vals, probs = self.group(quad, odd)
+                grad = self.stacked(d_ctx, at)
+                d_probs = mm_nt(grad, vals).astype(BF16).astype(F32)
+                d_vals.append(fold(mm_tn(probs.astype(BF16), grad)))
+                d_scores = probs * (d_probs - jnp.sum(probs * d_probs, axis=-1, keepdims=True))
+                d_scores = (jnp.where(self.causal, d_scores, 0.0) * self.head_dim ** -0.5).astype(BF16)
+                d_proj[:, pl.ds(at, 2 * self.head_dim)] = self.merged(mm(d_scores, keys)).astype(BF16)
+                d_keys.append(fold(mm_tn(d_scores, query)))
+            d_proj[:, pl.ds(self.dim + kv_at, 2 * self.head_dim)] = jnp.where(self.low, d_keys[0], d_keys[1]).astype(BF16)
+            d_proj[:, pl.ds(self.dim + self.kv + kv_at, 2 * self.head_dim)] = jnp.where(self.low, d_vals[0], d_vals[1]).astype(BF16)
+            return carry
+
+        lax.fori_loop(0, self.kv // (2 * self.head_dim), body, 0)
+
+
+def exchange_kernel(backward, head_dim, *refs):
+    if backward:
+        (rows_ref, u_ref, w1_ref, w3_ref, w2_ref, x_ref, n1_ref, n2_ref, wq_ref, wk_ref, wv_ref, wo_ref,
+         out_ref, gw1_ref, gw2_ref, gw3_ref, h_ref, norm_ref, proj, ctx, att_sem, got, own, stage, from_core, from_y, from_z, saved, acc1, acc2, acc3,
          own_sem, load_sem, store_sem, g_recv, g_core, g_y, g_z, s_core, r_core, s_y, r_y, s_z, r_z) = refs
     else:
-        (rows_ref, w1_ref, w3_ref, w2_ref, out_ref,
-         got, own, stage, from_core, from_y, from_z,
+        (rows_ref, w1_ref, w3_ref, w2_ref, x_ref, n1_ref, n2_ref, wq_ref, wk_ref, wv_ref, wo_ref, dy_ref, du_ref,
+         out_ref, dx_ref, gq_ref, gk_ref, gv_ref, go_ref, gn1_ref, gn2_ref, proj, ctx, att_sem, d_ctx, d_proj, got, own, stage, from_core, from_y, from_z,
          own_sem, g_recv, g_core, g_y, g_z, s_core, r_core, s_y, r_y, s_z, r_z) = refs
     tokens, dim = own.shape[1], own.shape[2]
     half = w1_ref.shape[0]
@@ -327,21 +405,71 @@
         for store in stores:
             store.start()
 
+    for n in range(4):
+        along_z(n, sent)
+        gather_to_y(n, me).wait_send()
+    for slot in range(8):
+        gather_to_core(slot, me).wait_send()
+    attention = Attention(got, proj, ctx, x_ref, n1_ref, n2_ref, head_dim)
+    weights = attention.copies(wq_ref, wk_ref, wv_ref, wo_ref, att_sem)
+    for copy in weights:
+        copy.start()
+
     def join(n):
         @pl.when(inside)
         def _():
             take_z(n, column(n))
             chain(n, start)
 
+    def pass_sum(n):
+        take_y(n)
+
+        @pl.when(at_end)
+        def _():
+            chain(n, start)
+
+    if not backward:
+        for copy in weights:
+            copy.wait()
+        attention.project()
+        attention.heads()
+        hid = attention.hidden()
+        d_norm, gn2_ref[...] = attention.norm_pull(hid.astype(F32), n2_ref, du_ref[...].astype(F32))
+        d_hid = (dy_ref[...].astype(F32) + d_norm.astype(F32)).astype(BF16)
+        dx_ref[...] = d_hid
+        for i in range(4):
+            d_ctx[:, i * attention.chunk:(i + 1) * attention.chunk] = mm_nt(d_hid, attention.weight(4 + i)).astype(BF16)
+        for i in range(4):
+            go_ref[pl.ds(i * attention.chunk, attention.chunk), :] = mm_tn(attention.part(ctx[...], i), d_hid).astype(BF16)
     join(3)
-    for n in (2, 1):
-        take_y(n)
-
-        @pl.when(at_end)
-        def _():
-            chain(n, start)
-
-        join(n)
+    if backward:
+        for copy in weights:
+            copy.wait()
+        attention.project()
+    pass_sum(2)
+    join(2)
+    if backward:
+        attention.heads()
+    else:
+        attention.pull_heads(d_ctx, d_proj)
+    pass_sum(1)
+    join(1)
+    kv = attention.kv
+    if backward:
+        hid = attention.hidden()
+        h_ref[...] = hid
+        norm_ref[...] = attention.norm(hid.astype(F32), n2_ref)
+    else:
+        rows = attention.normed()
+        for i in range(4):
+            block = pl.ds(i * attention.chunk, attention.chunk)
+            gq_ref[block, :] = mm_tn(attention.part(rows, i), d_proj[:, :dim]).astype(BF16)
+            gk_ref[block, :] = mm_tn(attention.part(rows, i), d_proj[:, dim:dim + kv]).astype(BF16)
+            gv_ref[block, :] = mm_tn(attention.part(rows, i), d_proj[:, dim + kv:]).astype(BF16)
+        pulled = [mm_nt(d_proj[:, :dim], attention.weight(i)) + mm_nt(d_proj[:, dim:], attention.weight(8 + i)) for i in range(4)]
+        d_rows = jnp.concatenate(pulled, axis=1).astype(BF16).astype(F32)
+        d_x, gn1_ref[...] = attention.norm_pull(x_ref[...].astype(F32), n1_ref, d_rows)
+        dx_ref[...] = (dx_ref[...].astype(F32) + d_x.astype(F32)).astype(BF16)
     take_y(0)
 
     @pl.when(z > 0)
@@ -356,11 +484,7 @@
     for n in (3, 2, 1):
         chain(n, sent)
     for n in range(4):
-        along_z(n, sent)
         send_y(n).wait_send()
-        gather_to_y(n, me).wait_send()
-    for slot in range(8):
-        gather_to_core(slot, me).wait_send()
     send_core(0).wait_send()
     send_core(1).wait_send()
     if backward:
@@ -368,13 +492,22 @@
             store.wait()
 
 
-def exchange(backward, rows, weights, tokens, saved=None):
+def exchange(backward, rows, weights, tokens, head_dim, sequence, saved=None):
     w_1, w_3, w_2 = weights
     dim = rows.shape[1]
     half, ff = w_1.shape[0], w_1.shape[2]
     dma = pltpu.SemaphoreType.DMA
     block = (tokens, dim)
+    model = (dim, dim)
+    narrow = (dim, dim // 2)
     scratch = [
+        pltpu.VMEM((tokens, 2 * dim), BF16),
+        pltpu.VMEM(block, BF16),
+        dma((16,)),
+    ]
+    if not backward:
+        scratch += [pltpu.VMEM(block, BF16), pltpu.VMEM((tokens, 2 * dim), BF16)]
+    scratch += [
         pltpu.VMEM((16,) + rows.shape, BF16),
         pltpu.VMEM((8,) + block, F32),
         pltpu.VMEM((2,) + block, F32),
@@ -394,18 +527,20 @@
             pltpu.VMEM((half, dim, ff), F32),
             dma(()), dma((2,)), dma((3,)),
         ]
-        operands = (rows, saved, w_1, w_3, w_2)
-        in_specs = [any_spec, any_spec, vmem_spec, vmem_spec, vmem_spec]
-        out_shape = [jax.ShapeDtypeStruct(block, BF16), jax.ShapeDtypeStruct((half, dim, ff), F32), jax.ShapeDtypeStruct((half, ff, dim), F32), jax.ShapeDtypeStruct((half, dim, ff), F32)]
-        out_specs = [vmem_spec, any_spec, any_spec, any_spec]
+        operands = (rows, saved, w_1, w_3, w_2) + sequence
+        in_specs = [any_spec, any_spec] + [vmem_spec] * 6 + [any_spec] * 4
+        out_shape = [jax.ShapeDtypeStruct(block, BF16), jax.ShapeDtypeStruct((half, dim, ff), F32), jax.ShapeDtypeStruct((half, ff, dim), F32), jax.ShapeDtypeStruct((half, dim, ff), F32), jax.ShapeDtypeStruct(block, BF16), jax.ShapeDtypeStruct(block, BF16)]
+        out_specs = [vmem_spec, any_spec, any_spec, any_spec, vmem_spec, vmem_spec]
     else:
         scratch += [dma(())]
-        operands = (rows, w_1, w_3, w_2)
-        in_specs = [any_spec, vmem_spec, vmem_spec, vmem_spec]
-        out_shape = [jax.ShapeDtypeStruct(block, F32)]
-        out_specs = [vmem_spec]
+        operands = (rows, w_1, w_3, w_2) + sequence
+        in_specs = [any_spec] + [vmem_spec] * 6 + [any_spec] * 4 + [vmem_spec] * 2
+        out_shape = [jax.ShapeDtypeStruct(block, F32), jax.ShapeDtypeStruct(block, BF16)]
+        out_shape += [jax.ShapeDtypeStruct(shape, BF16) for shape in (model, narrow, narrow, model)]
+        out_shape += [jax.ShapeDtypeStruct((1, dim), F32)] * 2
+        out_specs = [vmem_spec] * 8
     return pl.pallas_call(
-        functools.partial(exchange_kernel, backward),
+        functools.partial(exchange_kernel, backward, head_dim),
         out_shape=out_shape,
         in_specs=in_specs,
         out_specs=out_specs,
@@ -415,16 +550,6 @@
     )(*operands)
 
 
-def device_backward(x_dev, dy_dev, du_dev, norm_1, norm_2, w_q, w_k, w_v, w_o):
-    attn_val, attn_pull = jax.vjp(attn_out, x_dev, norm_1, w_q, w_k, w_v, w_o)
-    h_dev = add_rows(x_dev, attn_val)
-    _, norm_pull = jax.vjp(rms_norm, h_dev, norm_2)
-    dh_norm, grad_n2 = norm_pull(du_dev)
-    dh_dev = add_rows(dy_dev, dh_norm)
-    grad_x, grad_n1, grad_q, grad_k, grad_v, grad_o = attn_pull(dh_dev)
-    return (add_rows(dh_dev, grad_x), grad_q.astype(jnp.float32), grad_k.astype(jnp.float32), grad_v.astype(jnp.float32), grad_o.astype(jnp.float32), grad_n1.astype(jnp.float32), grad_n2.astype(jnp.float32))
-
-
 def solution(mesh):
     group = mesh.shape['expert']
 
@@ -443,12 +568,13 @@
             return jnp.concatenate([rows, table], axis=0)
 
         weights = (w_1, w_3, w_2)
-        du_rows, grad_w1, grad_w2, grad_w3 = exchange(True, with_routing(dy_b, eid_b, slot_b, gate_b), weights, tokens, u_b)
-        h_a = add_rows(x_a, attn_out(x_a, norm_1, w_q, w_k, w_v, w_o))
-        u_a = rms_norm(h_a, norm_2)
-        mixed = exchange(False, with_routing(u_a, eid_a, slot_a, gate_a), weights, tokens)[0]
+        head_dim = w_q.shape[2]
+        layer = (norm_1[None], norm_2[None], w_q.reshape(model_dim, -1), w_k.reshape(model_dim, -1), w_v.reshape(model_dim, -1), w_o.reshape(-1, model_dim))
+        du_rows, grad_w1, grad_w2, grad_w3, h_a, u_a = exchange(True, with_routing(dy_b, eid_b, slot_b, gate_b), weights, tokens, head_dim, (x_a,) + layer, u_b)
+        mixed, dx_b, g_q, g_k, g_v, g_o, g_n1, g_n2 = exchange(False, with_routing(u_a, eid_a, slot_a, gate_a), weights, tokens, head_dim, (x_b,) + layer + (dy_b, du_rows))
         y_a = (h_a.astype(jnp.float32) + mixed).astype(jnp.bfloat16)
-        dx_b, g_q, g_k, g_v, g_o, g_n1, g_n2 = device_backward(x_b, dy_b, du_rows, norm_1, norm_2, w_q, w_k, w_v, w_o)
+        g_q, g_k, g_v, g_o = (grad.astype(jnp.float32).reshape(weight.shape) for grad, weight in ((g_q, w_q), (g_k, w_k), (g_v, w_v), (g_o, w_o)))
+        g_n1, g_n2 = g_n1[0], g_n2[0]
         return (y_a, dx_b, grad_w1, grad_w2, grad_w3, g_q[None], g_k[None], g_v[None], g_o[None], g_n1[None], g_n2[None])
 
     row_spec = P(('data', 'expert'), None)

time: 387 us -> 369 us (0.953)
  matrix products: 32.9 us -> 0 us
  local copies, waits for them, and re-layouts: 11.9 us -> 29.4 us
  other arithmetic: 25.5 us -> 16 us
  Pallas kernels: 315 us -> 322 us
    dot_general x14 -> x0, matrix products: 17.2 us -> none  [the longest x4 7.62 us: attn_out(): jnp.einsum('the,hed->td', context, w_o, preferred_element_type=jnp.float32)]
    unnamed x9 -> x0, matrix products: 10.9 us -> none
    pallas_call x2, Pallas kernels: 315 us -> 322 us  [exchange(): pl.pallas_call(functools.partial(exchange_kernel, backward, head_dim), ou...]
    another operation x0 -> x3, local copies, waits for them, and re-layouts: none -> 7.23 us  [the longest x1 2.98 us: local_step(): g_q[None]]
    reshape x0 -> x3, local copies, waits for them, and re-layouts: none -> 6.65 us  [the longest x1 4.02 us: local_step(): w_q.reshape(model_dim, -1)]
    convert_element_type x7 -> x0, other arithmetic: 5.25 us -> none  [the longest x2 2.41 us: add_rows(): (first.astype(jnp.float32) + second.astype(jnp.float32)).astype(jnp.bfloa...]
    broadcast_in_dim x3 -> x0, other arithmetic: 5.23 us -> none  [the longest x1 2.32 us: local_step(): g_q[None]]
    reduce_sum x4 -> x0, other arithmetic: 5.13 us -> none  [the longest x2 2.45 us: rms_norm(): jnp.mean(wide * wide, axis=-1, keepdims=True) + NORM_EPS]
where the time goes in v4:
time: 369 us; the launch traced here: 368 us
  Pallas kernels  322 us (87%)
  local copies, waits for them, and re-layouts  29.4 us (8%)
  other arithmetic  16 us (4%)
    pallas_call x2, Pallas kernels, exchange(): pl.pallas_call(functools.partial(exchange_kernel, backward, head_dim), ou...  322 us
    unnamed x30, local copies, waits for them, and re-layouts  12.8 us

profile of v4, /device:TPU:0, one launch (start us, length us, event | category | flops | bytes accessed | tf_op | source)
XLA Modules:
  0.0 368.2 jit_solution(12773354386474612414)
XLA Ops:
  2.0 0.8 select_reduce_fusion
  3.5 0.8 select_reduce_fusion.1
  5.8 0.8 select_reduce_fusion.2
  7.3 0.8 select_reduce_fusion.3
  8.1 1.9 pad_maximum_fusion.refs_0_
  10.0 1.3 broadcast_in_dim.56.refs_6_.refs_5_
  11.3 1.3 broadcast_in_dim.57.refs_7_.refs_6_
  12.6 4.0 %copy.63.refs_8_.refs_7_ = bf16[1024,1024]{1,0:T(8,128)(2,1)} copy(bf16[1024,1024]{0,1:T(8,128)(2,1)} %bitcast.31) | data formatting | bytes 4194304 | tf_op jit(solution)/shard_map/reshape | solution.py:572
  16.6 1.3 copy.64.refs_9_.refs_8_
  17.9 1.3 copy.65.refs_10_.refs_9_
  19.2 162.9 %exchange_b.1 = (bf16[256,1024]{1,0:T(8,128)(2,1)}, f32[2,1024,512]{2,1,0:T(8,128)}, f32[2,512,1024]{2,1,0:T(8,128)}, f32[2,1024,512]{2,1,0:T(8,128)}, bf16[256,...) custom-call(bf16[272,1024]{1,0:T(8,128)(2,1)} %pad_maximum_fusion.refs_0_, bf16[2,2048,1024]{2,1,0:T(8,128)(2,1)} %refs_1_.2, ...), custom_call_target="tpu_custom_call" | custom-call | tf_op jit(solution)/shard_map/exchange_b/pallas_call | solution.py:542
  182.1 1.9 pad_maximum_fusion.1.refs_0_
  184.0 159.2 %exchange_a.1 = (f32[256,1024]{1,0:T(8,128)}, bf16[256,1024]{1,0:T(8,128)(2,1)}, bf16[1024,1024]{1,0:T(8,128)(2,1)}, bf16[1024,512]{1,0:T(8,128)(2,1)}, bf16[102...) custom-call(bf16[272,1024]{1,0:T(8,128)(2,1)} %pad_maximum_fusion.1.refs_0_, ...), custom_call_target="tpu_custom_call" | custom-call | tf_op jit(solution)/shard_map/exchange_a/pallas_call | solution.py:542
  343.2 2.3 add_convert_fusion
  345.6 3.0 copy.71
  348.5 2.7 copy.72
  351.2 1.6 copy.73
  353.6 2.6 convert.4
  356.2 0.8 copy.80
  357.6 2.1 copy.81
  359.7 1.6 copy-done.1
  361.3 2.1 copy.82
  363.4 1.6 copy-done
  365.0 2.0 copy.83
  (40 shorter events, 7.0 us)
Async XLA Ops:
  12.6 4.0 %copy-start.6 = (bf16[1024,8,64]{0,2,1:T(8,128)(2,1)S(1)}, bf16[1024,8,64]{0,2,1:T(8,128)(2,1)}, u32[]{:S(2)}) copy-start(bf16[1024,8,64]{0,2,1:T(8,128)(2,1)} %param.32) | copy-start | bytes 3145732
  16.6 1.3 copy-start.7
  184.0 159.2 %copy-start.9 = (bf16[256,1024]{1,0:T(8,128)(2,1)S(1)}, bf16[256,1024]{1,0:T(8,128)(2,1)}, u32[]{:S(2)}) copy-start(bf16[256,1024]{1,0:T(8,128)(2,1)} %get-tuple-element.25) | copy-start | bytes 1572868
  343.2 2.4 copy-start.4
  348.5 2.7 copy-start.5
  351.2 2.3 copy-start.3
  353.5 2.6 copy-start.8
  353.6 4.1 %copy-start.2 = (f32[2,1024,512]{2,1,0:T(8,128)S(1)}, f32[2,1024,512]{2,1,0:T(8,128)}, u32[]{:S(2)}) copy-start(f32[2,1024,512]{2,1,0:T(8,128)} %get-tuple-element.63) | copy-start | bytes 12582916
  357.6 3.7 %copy-start.1 = (f32[2,512,1024]{2,1,0:T(8,128)S(1)}, f32[2,512,1024]{2,1,0:T(8,128)}, u32[]{:S(2)}) copy-start(f32[2,512,1024]{2,1,0:T(8,128)} %get-tuple-element.64) | copy-start | bytes 12582916
  361.3 3.7 %copy-start = (f32[2,1024,512]{2,1,0:T(8,128)S(1)}, f32[2,1024,512]{2,1,0:T(8,128)}, u32[]{:S(2)}) copy-start(f32[2,1024,512]{2,1,0:T(8,128)} %get-tuple-element.65) | copy-start | bytes 12582916
  365.0 2.0 copy-start.11
  365.0 2.6 copy-start.10

commit v5 on v4

--- a/solution.py
+++ b/solution.py
@@ -10,15 +10,9 @@
 F32 = jnp.float32
 BF16 = jnp.bfloat16
 VMEM_BYTES = 66_000_000
+SIDE = 4
 
 NORM_EPS = 1e-6
-
-
-def routing_table(expert_ids, slot_ids, gates, experts):
-    hit = (expert_ids[:, :, None] == jnp.arange(experts)[None, None, :]) & (slot_ids >= 0)[:, :, None]
-    slots = jnp.sum(jnp.where(hit, slot_ids[:, :, None] + 1, 0), axis=1) - 1
-    weights = jnp.sum(jnp.where(hit, gates.astype(jnp.float32)[:, :, None], 0.0), axis=1)
-    return slots.astype(jnp.bfloat16), weights.astype(jnp.bfloat16)
 
 
 def mm(left, right):
@@ -34,8 +28,8 @@
 
 
 class Attention:
-    def __init__(self, got, proj, ctx, x_ref, n1_ref, n2_ref, head_dim):
-        self.got, self.proj, self.ctx, self.x_ref, self.n1_ref, self.n2_ref = got, proj, ctx, x_ref, n1_ref, n2_ref
+    def __init__(self, got, proj, ctx, x_ref, gain_1, gain_2, head_dim):
+        self.got, self.proj, self.ctx, self.x_ref, self.gain_1, self.gain_2 = got, proj, ctx, x_ref, gain_1, gain_2
         self.tokens, self.dim = x_ref.shape
         self.head_dim = head_dim
         self.kv = self.dim // 2
@@ -61,18 +55,18 @@
     def scale(self, wide):
         return lax.rsqrt(jnp.mean(wide * wide, axis=-1, keepdims=True) + NORM_EPS)
 
-    def norm(self, wide, gain_ref):
-        return (wide * self.scale(wide) * gain_ref[...].astype(F32)).astype(BF16)
-
-    def norm_pull(self, wide, gain_ref, grad):
+    def norm(self, wide, gain):
+        return (wide * self.scale(wide) * gain).astype(BF16)
+
+    def norm_pull(self, wide, gain, grad):
         inv = self.scale(wide)
         gain_grad = jnp.sum(grad * (wide * inv), axis=0, keepdims=True).astype(BF16).astype(F32)
-        inner = grad * gain_ref[...].astype(F32)
+        inner = grad * gain
         row_grad = inv * inner - wide * (inv * inv * inv * jnp.mean(inner * wide, axis=-1, keepdims=True))
         return row_grad.astype(BF16), gain_grad
 
     def normed(self):
-        return self.norm(self.x_ref[...].astype(F32), self.n1_ref)
+        return self.norm(self.x_ref[...].astype(F32), self.gain_1)
 
     def part(self, rows, i):
         return rows[:, i * self.chunk:(i + 1) * self.chunk]
@@ -140,17 +134,19 @@
         lax.fori_loop(0, self.kv // (2 * self.head_dim), body, 0)
 
 
-def exchange_kernel(backward, head_dim, *refs):
-    if backward:
-        (rows_ref, u_ref, w1_ref, w3_ref, w2_ref, x_ref, n1_ref, n2_ref, wq_ref, wk_ref, wv_ref, wo_ref,
+def exchange_kernel(backward, head_dim, choices, *refs):
+    if backward:
+        (rows_ref, u_ref, w1_ref, w3_ref, w2_ref, x_ref, wq_ref, wk_ref, wv_ref, wo_ref,
          out_ref, gw1_ref, gw2_ref, gw3_ref, h_ref, norm_ref, proj, ctx, att_sem, got, own, stage, from_core, from_y, from_z, saved, acc1, acc2, acc3,
-         own_sem, load_sem, store_sem, g_recv, g_core, g_y, g_z, s_core, r_core, s_y, r_y, s_z, r_z) = refs
+         own_sem, load_sem, store_sem, side_z, side_y, sz_send, sz_recv, sy_send, sy_recv, g_recv, g_core, g_y, g_z, s_core, r_core, s_y, r_y, s_z, r_z) = refs
     else:
-        (rows_ref, w1_ref, w3_ref, w2_ref, x_ref, n1_ref, n2_ref, wq_ref, wk_ref, wv_ref, wo_ref, dy_ref, du_ref,
+        (rows_ref, w1_ref, w3_ref, w2_ref, x_ref, wq_ref, wk_ref, wv_ref, wo_ref, dy_ref, du_ref,
          out_ref, dx_ref, gq_ref, gk_ref, gv_ref, go_ref, gn1_ref, gn2_ref, proj, ctx, att_sem, d_ctx, d_proj, got, own, stage, from_core, from_y, from_z,
-         own_sem, g_recv, g_core, g_y, g_z, s_core, r_core, s_y, r_y, s_z, r_z) = refs
+         own_sem, side_z, side_y, sz_send, sz_recv, sy_send, sy_recv, g_recv, g_core, g_y, g_z, s_core, r_core, s_y, r_y, s_z, r_z) = refs
     tokens, dim = own.shape[1], own.shape[2]
     half = w1_ref.shape[0]
+    main = dim - dim // SIDE
+    first, last = pl.ds(0, main), pl.ds(main, dim - main)
     me = lax.axis_index('expert')
     z, y, c = lax.div(me, 4), lax.rem(lax.div(me, 2), 2), lax.rem(me, 2)
 
@@ -245,15 +241,17 @@
     else:
         slots = tokens // 2
 
-    sel = (lax.broadcasted_iota(jnp.int32, (16, 16), 1) == me).astype(BF16)
     slot_row = lax.broadcasted_iota(jnp.int32, (slots, tokens), 0).astype(F32)
 
     def masks(block):
-        table = mm(sel, got[block, tokens:, :])
+        facts = got[block, tokens:, :].astype(F32)
+        ids, slot_ids, gates = (facts[:choices, i * tokens:(i + 1) * tokens] for i in range(3))
         plain, gated = [], []
         for e in range(half):
-            hit = table[0:1, e * tokens:(e + 1) * tokens] == slot_row
-            gate = table[0:1, (half + e) * tokens:(half + e + 1) * tokens]
+            kept = jnp.logical_and(ids == (me * half + e).astype(F32), slot_ids >= 0.0)
+            slot = jnp.sum(jnp.where(kept, slot_ids + 1.0, 0.0), axis=0, keepdims=True) - 1.0
+            gate = jnp.sum(jnp.where(kept, gates, 0.0), axis=0, keepdims=True)
+            hit = slot == slot_row
             plain.append(jnp.where(hit, 1.0, 0.0).astype(BF16))
             gated.append(jnp.where(hit, gate, 0.0).astype(BF16))
         return jnp.concatenate(plain, axis=0), jnp.concatenate(gated, axis=0)
@@ -304,30 +302,63 @@
         return remote(stage.at[which], from_core.at[which], s_core.at[which], r_core.at[which], other_core)
 
     def send_y(n):
-        return remote(own.at[4 + n], from_y.at[n], s_y.at[n], r_y.at[n], other_y)
+        return remote(own.at[4 + n, :, first], from_y.at[n], s_y.at[n], r_y.at[n], other_y)
 
     def take_y(n):
         send_y(n).wait_recv()
-        own[n] += from_y[n]
+        own[n, :, :main] += from_y[n]
+
+    def hop(n, source, landing, base, send, recv, action):
+        goal = column(n)
+
+        @pl.when(goal > z)
+        def _():
+            action(remote(source, landing.at[base + goal], send, recv.at[base + goal], right))
+
+        @pl.when(goal == z - 1)
+        def _():
+            action(remote(source, landing.at[base + 4], send, recv.at[base + 4], left))
+
+        @pl.when(goal < z - 1)
+        def _():
+            action(remote(source, landing.at[base + goal], send, recv.at[base + goal], left))
 
     def chain(n, action):
-        goal = column(n)
-
-        @pl.when(goal > z)
-        def _():
-            action(remote(own.at[n], from_z.at[goal], s_z.at[n - 1], r_z.at[goal], right))
-
-        @pl.when(goal == z - 1)
-        def _():
-            action(remote(own.at[n], from_z.at[4], s_z.at[n - 1], r_z.at[4], left))
-
-        @pl.when(goal < z - 1)
-        def _():
-            action(remote(own.at[n], from_z.at[goal], s_z.at[n - 1], r_z.at[goal], left))
+        hop(n, own.at[n, :, first], from_z, 0, s_z.at[n - 1], r_z, action)
 
     def take_z(n, slot):
-        remote(own.at[n], from_z.at[slot], s_z.at[0], r_z.at[slot], left).wait_recv()
-        own[n] += from_z[slot]
+        remote(own.at[n, :, first], from_z.at[slot], s_z.at[0], r_z.at[slot], left).wait_recv()
+        own[n, :, :main] += from_z[slot]
+
+    def side_chain(across, n, action):
+        hop(n, own.at[4 * across + n, :, last], side_z, 5 * across, sz_send.at[3 * across + n - 1], sz_recv, action)
+
+    def side_take(across, n, slot):
+        at_slot = 5 * across + slot
+        remote(own.at[n, :, last], side_z.at[at_slot], sz_send.at[0], sz_recv.at[at_slot], left).wait_recv()
+        own[4 * across + n, :, main:] += side_z[at_slot]
+
+    def side_cross():
+        return remote(own.at[4, :, last], side_y, sy_send, sy_recv, other_y)
+
+    def at_steps(step, who, table, action):
+        for when, across, n in table:
+            @pl.when(jnp.logical_and(who, step == when))
+            def _():
+                action(across, n)
+
+    def side_join(across, n):
+        side_take(across, n, column(n))
+        side_chain(across, n, start)
+
+    def side_gather(across):
+        @pl.when(z > 0)
+        def _():
+            side_take(across, 0, z)
+
+        @pl.when(z < 3)
+        def _():
+            side_take(across, 0, 4)
 
     def step_body(step, carry):
         n, across = order(step)
@@ -389,6 +420,9 @@
         def _():
             send_y(n).start()
 
+        at_steps(step, at_end, ((1, 0, 1), (2, 0, 2), (3, 0, 3), (4, 1, 3), (5, 1, 2), (6, 1, 1)), lambda across, n: side_chain(across, n, start))
+        at_steps(step, inside, ((4, 0, 2), (5, 0, 3), (6, 0, 1), (6, 1, 3), (7, 1, 2), (7, 1, 1)), side_join)
+
         @pl.when(step == 6)
         def _():
             take_y(3)
@@ -410,7 +444,8 @@
         gather_to_y(n, me).wait_send()
     for slot in range(8):
         gather_to_core(slot, me).wait_send()
-    attention = Attention(got, proj, ctx, x_ref, n1_ref, n2_ref, head_dim)
+    gains = got[me, tokens:, :].astype(F32)
+    attention = Attention(got, proj, ctx, x_ref, gains[choices:choices + 1], gains[choices + 1:choices + 2], head_dim)
     weights = attention.copies(wq_ref, wk_ref, wv_ref, wo_ref, att_sem)
     for copy in weights:
         copy.start()
@@ -434,7 +469,7 @@
         attention.project()
         attention.heads()
         hid = attention.hidden()
-        d_norm, gn2_ref[...] = attention.norm_pull(hid.astype(F32), n2_ref, du_ref[...].astype(F32))
+        d_norm, gn2_ref[...] = attention.norm_pull(hid.astype(F32), attention.gain_2, du_ref[...].astype(F32))
         d_hid = (dy_ref[...].astype(F32) + d_norm.astype(F32)).astype(BF16)
         dx_ref[...] = d_hid
         for i in range(4):
@@ -452,13 +487,15 @@
         attention.heads()
     else:
         attention.pull_heads(d_ctx, d_proj)
+    side_gather(1)
+    side_cross().start()
     pass_sum(1)
     join(1)
     kv = attention.kv
     if backward:
         hid = attention.hidden()
         h_ref[...] = hid
-        norm_ref[...] = attention.norm(hid.astype(F32), n2_ref)
+        norm_ref[...] = attention.norm(hid.astype(F32), attention.gain_2)
     else:
         rows = attention.normed()
         for i in range(4):
@@ -468,9 +505,12 @@
             gv_ref[block, :] = mm_tn(attention.part(rows, i), d_proj[:, dim + kv:]).astype(BF16)
         pulled = [mm_nt(d_proj[:, :dim], attention.weight(i)) + mm_nt(d_proj[:, dim:], attention.weight(8 + i)) for i in range(4)]
         d_rows = jnp.concatenate(pulled, axis=1).astype(BF16).astype(F32)
-        d_x, gn1_ref[...] = attention.norm_pull(x_ref[...].astype(F32), n1_ref, d_rows)
+        d_x, gn1_ref[...] = attention.norm_pull(x_ref[...].astype(F32), attention.gain_1, d_rows)
         dx_ref[...] = (dx_ref[...].astype(F32) + d_x.astype(F32)).astype(BF16)
+    side_gather(0)
     take_y(0)
+    side_cross().wait_recv()
+    own[0, :, main:] += side_y[...]
 
     @pl.when(z > 0)
     def _():
@@ -483,6 +523,9 @@
     out_ref[...] = own[0].astype(out_ref.dtype)
     for n in (3, 2, 1):
         chain(n, sent)
+        side_chain(0, n, sent)
+        side_chain(1, n, sent)
+    side_cross().wait_send()
     for n in range(4):
         send_y(n).wait_send()
     send_core(0).wait_send()
@@ -492,7 +535,7 @@
             store.wait()
 
 
-def exchange(backward, rows, weights, tokens, head_dim, sequence, saved=None):
+def exchange(backward, rows, weights, tokens, head_dim, choices, sequence, saved=None):
     w_1, w_3, w_2 = weights
     dim = rows.shape[1]
     half, ff = w_1.shape[0], w_1.shape[2]
@@ -512,10 +555,10 @@
         pltpu.VMEM((8,) + block, F32),
         pltpu.VMEM((2,) + block, F32),
         pltpu.VMEM((2,) + block, F32),
-        pltpu.VMEM((4,) + block, F32),
-        pltpu.VMEM((5,) + block, F32),
+        pltpu.VMEM((4, tokens, dim - dim // SIDE), F32),
+        pltpu.VMEM((5, tokens, dim - dim // SIDE), F32),
     ]
-    tail = [dma((16,)), dma((8,)), dma((4,)), dma((5,)), dma((2,)), dma((2,)), dma((4,)), dma((4,)), dma((3,)), dma((5,))]
+    tail = [pltpu.VMEM((10, tokens, dim // SIDE), F32), pltpu.VMEM((tokens, dim // SIDE), F32), dma((6,)), dma((10,)), dma(()), dma(()), dma((16,)), dma((8,)), dma((4,)), dma((5,)), dma((2,)), dma((2,)), dma((4,)), dma((4,)), dma((3,)), dma((5,))]
     any_spec = pl.BlockSpec(memory_space=pl.ANY)
     vmem_spec = pl.BlockSpec(memory_space=pltpu.VMEM)
     if backward:
@@ -528,19 +571,19 @@
             dma(()), dma((2,)), dma((3,)),
         ]
         operands = (rows, saved, w_1, w_3, w_2) + sequence
-        in_specs = [any_spec, any_spec] + [vmem_spec] * 6 + [any_spec] * 4
+        in_specs = [any_spec, any_spec] + [vmem_spec] * 4 + [any_spec] * 4
         out_shape = [jax.ShapeDtypeStruct(block, BF16), jax.ShapeDtypeStruct((half, dim, ff), F32), jax.ShapeDtypeStruct((half, ff, dim), F32), jax.ShapeDtypeStruct((half, dim, ff), F32), jax.ShapeDtypeStruct(block, BF16), jax.ShapeDtypeStruct(block, BF16)]
         out_specs = [vmem_spec, any_spec, any_spec, any_spec, vmem_spec, vmem_spec]
     else:
         scratch += [dma(())]
         operands = (rows, w_1, w_3, w_2) + sequence
-        in_specs = [any_spec] + [vmem_spec] * 6 + [any_spec] * 4 + [vmem_spec] * 2
+        in_specs = [any_spec] + [vmem_spec] * 4 + [any_spec] * 4 + [vmem_spec] * 2
         out_shape = [jax.ShapeDtypeStruct(block, F32), jax.ShapeDtypeStruct(block, BF16)]
         out_shape += [jax.ShapeDtypeStruct(shape, BF16) for shape in (model, narrow, narrow, model)]
         out_shape += [jax.ShapeDtypeStruct((1, dim), F32)] * 2
         out_specs = [vmem_spec] * 8
     return pl.pallas_call(
-        functools.partial(exchange_kernel, backward, head_dim),
+        functools.partial(exchange_kernel, backward, head_dim, choices),
         out_shape=out_shape,
         in_specs=in_specs,
         out_specs=out_specs,
@@ -555,23 +598,22 @@
 
     def local_step(x_a, x_b, dy_b, eid_a, slot_a, gate_a, eid_b, slot_b, gate_b, u_b, norm_1, norm_2, w_q, w_k, w_v, w_o, w_1, w_2, w_3):
         local_experts = w_1.shape[0]
-        experts = local_experts * group
         model_dim = x_a.shape[1]
 
         tokens = x_a.shape[0]
 
         def with_routing(rows, expert_ids, slot_ids, gates):
-            slots, weights = routing_table(expert_ids, slot_ids, gates, experts)
-            table = jnp.stack([slots, weights], axis=1).reshape(tokens, 2, group, local_experts)
-            table = table.transpose(2, 1, 3, 0).reshape(group, 2 * local_experts * tokens)
-            table = jnp.pad(table, ((0, 0), (0, model_dim - table.shape[1])))
+            facts = jnp.concatenate([array.astype(jnp.bfloat16).T for array in (expert_ids, slot_ids, gates)], axis=1)
+            facts = jnp.pad(facts, ((0, 0), (0, model_dim - facts.shape[1])))
+            table = jnp.concatenate([facts, norm_1[None], norm_2[None]], axis=0)
+            table = jnp.pad(table, ((0, 16 - table.shape[0]), (0, 0)))
             return jnp.concatenate([rows, table], axis=0)
 
         weights = (w_1, w_3, w_2)
         head_dim = w_q.shape[2]
-        layer = (norm_1[None], norm_2[None], w_q.reshape(model_dim, -1), w_k.reshape(model_dim, -1), w_v.reshape(model_dim, -1), w_o.reshape(-1, model_dim))
-        du_rows, grad_w1, grad_w2, grad_w3, h_a, u_a = exchange(True, with_routing(dy_b, eid_b, slot_b, gate_b), weights, tokens, head_dim, (x_a,) + layer, u_b)
-        mixed, dx_b, g_q, g_k, g_v, g_o, g_n1, g_n2 = exchange(False, with_routing(u_a, eid_a, slot_a, gate_a), weights, tokens, head_dim, (x_b,) + layer + (dy_b, du_rows))
+        layer = (w_q.reshape(model_dim, -1), w_k.reshape(model_dim, -1), w_v.reshape(model_dim, -1), w_o.reshape(-1, model_dim))
+        du_rows, grad_w1, grad_w2, grad_w3, h_a, u_a = exchange(True, with_routing(dy_b, eid_b, slot_b, gate_b), weights, tokens, head_dim, eid_b.shape[1], (x_a,) + layer, u_b)
+        mixed, dx_b, g_q, g_k, g_v, g_o, g_n1, g_n2 = exchange(False, with_routing(u_a, eid_a, slot_a, gate_a), weights, tokens, head_dim, eid_a.shape[1], (x_b,) + layer + (dy_b, du_rows))
         y_a = (h_a.astype(jnp.float32) + mixed).astype(jnp.bfloat16)
         g_q, g_k, g_v, g_o = (grad.astype(jnp.float32).reshape(weight.shape) for grad, weight in ((g_q, w_q), (g_k, w_k), (g_v, w_v), (g_o, w_o)))
         g_n1, g_n2 = g_n1[0], g_n2[0]

time: 369 us -> 337 us (0.913)
  Pallas kernels: 322 us -> 296 us
  other arithmetic: 16 us -> 11.5 us
    pallas_call x2, Pallas kernels: 322 us -> 296 us  [exchange(): pl.pallas_call(functools.partial(exchange_kernel, backward, head_dim, cho...]
where the time goes in v5:
time: 337 us; the launch traced here: 336 us
  Pallas kernels  296 us (88%)
  local copies, waits for them, and re-layouts  28.1 us (8%)
  other arithmetic  11.5 us (3%)
    pallas_call x2, Pallas kernels, exchange(): pl.pallas_call(functools.partial(exchange_kernel, backward, head_dim, cho...  296 us
    unnamed x30, local copies, waits for them, and re-layouts  12.8 us

profile of v5, /device:TPU:0, one launch (start us, length us, event | category | flops | bytes accessed | tf_op | source)
XLA Modules:
  0.0 336.0 jit_solution(2834756940103967811)
XLA Ops:
  0.6 0.7 broadcast_in_dim.9
  2.0 0.7 convert_bitcast_fusion.2
  2.7 0.7 fusion.11
  3.4 0.7 convert_bitcast_fusion
  4.1 0.7 fusion.13
  4.8 1.9 fusion.2.refs_0_
  6.7 4.0 %copy.36.refs_6_.refs_5_ = bf16[1024,1024]{1,0:T(8,128)(2,1)} copy(bf16[1024,1024]{0,1:T(8,128)(2,1)} %bitcast.25) | data formatting | bytes 4194304 | tf_op jit(solution)/shard_map/reshape | solution.py:614
  10.8 1.3 copy.37.refs_7_.refs_6_
  12.1 1.3 copy.38.refs_8_.refs_7_
  13.4 150.6 %exchange_b.1 = (bf16[256,1024]{1,0:T(8,128)(2,1)}, f32[2,1024,512]{2,1,0:T(8,128)}, f32[2,512,1024]{2,1,0:T(8,128)}, f32[2,1024,512]{2,1,0:T(8,128)}, bf16[256,...) custom-call(bf16[272,1024]{1,0:T(8,128)(2,1)} %fusion.2.refs_0_, bf16[2,2048,1024]{2,1,0:T(8,128)(2,1)} %refs_1_.2, ...), custom_call_target="tpu_custom_call" | custom-call | tf_op jit(solution)/shard_map/exchange_b/pallas_call | solution.py:585
  164.0 1.9 fusion.3.refs_0_
  165.9 145.1 %exchange_a.1 = (f32[256,1024]{1,0:T(8,128)}, bf16[256,1024]{1,0:T(8,128)(2,1)}, bf16[1024,1024]{1,0:T(8,128)(2,1)}, bf16[1024,512]{1,0:T(8,128)(2,1)}, bf16[102...) custom-call(bf16[272,1024]{1,0:T(8,128)(2,1)} %fusion.3.refs_0_, ...), custom_call_target="tpu_custom_call" | custom-call | tf_op jit(solution)/shard_map/exchange_a/pallas_call | solution.py:585
  311.1 2.3 add_convert_fusion
  313.4 3.0 copy.42
  316.4 2.7 copy.43
  319.0 1.6 copy.44
  320.6 0.7 copy-done.3
  321.4 2.6 convert.4
  324.0 0.8 copy.51
  325.4 2.1 copy.52
  327.6 1.6 copy-done.1
  329.1 2.1 copy.53
  331.3 1.6 copy-done
  332.8 2.0 copy.54
  (25 shorter events, 2.6 us)
Async XLA Ops:
  6.7 4.0 %copy-start.6 = (bf16[1024,8,64]{0,2,1:T(8,128)(2,1)S(1)}, bf16[1024,8,64]{0,2,1:T(8,128)(2,1)}, u32[]{:S(2)}) copy-start(bf16[1024,8,64]{0,2,1:T(8,128)(2,1)} %param.32) | copy-start | bytes 3145732
  10.8 1.3 copy-start.7
  165.9 145.2 %copy-start.9 = (bf16[256,1024]{1,0:T(8,128)(2,1)S(1)}, bf16[256,1024]{1,0:T(8,128)(2,1)}, u32[]{:S(2)}) copy-start(bf16[256,1024]{1,0:T(8,128)(2,1)} %get-tuple-element.25) | copy-start | bytes 1572868
  311.0 2.4 copy-start.4
  316.4 2.7 copy-start.5
  319.0 2.3 copy-start.3
  321.4 2.6 copy-start.8
  321.4 4.1 %copy-start.2 = (f32[2,1024,512]{2,1,0:T(8,128)S(1)}, f32[2,1024,512]{2,1,0:T(8,128)}, u32[]{:S(2)}) copy-start(f32[2,1024,512]{2,1,0:T(8,128)} %get-tuple-element.69) | copy-start | bytes 12582916
  325.4 3.7 %copy-start.1 = (f32[2,512,1024]{2,1,0:T(8,128)S(1)}, f32[2,512,1024]{2,1,0:T(8,128)}, u32[]{:S(2)}) copy-start(f32[2,512,1024]{2,1,0:T(8,128)} %get-tuple-element.70) | copy-start | bytes 12582916
  329.1 3.7 %copy-start = (f32[2,1024,512]{2,1,0:T(8,128)S(1)}, f32[2,1024,512]{2,1,0:T(8,128)}, u32[]{:S(2)}) copy-start(f32[2,1024,512]{2,1,0:T(8,128)} %get-tuple-element.71) | copy-start | bytes 12582916
  332.8 2.0 copy-start.11
  332.8 2.6 copy-start.10

commit v6 on v5

--- a/solution.py
+++ b/solution.py
@@ -141,7 +141,7 @@
          own_sem, load_sem, store_sem, side_z, side_y, sz_send, sz_recv, sy_send, sy_recv, g_recv, g_core, g_y, g_z, s_core, r_core, s_y, r_y, s_z, r_z) = refs
     else:
         (rows_ref, w1_ref, w3_ref, w2_ref, x_ref, wq_ref, wk_ref, wv_ref, wo_ref, dy_ref, du_ref,
-         out_ref, dx_ref, gq_ref, gk_ref, gv_ref, go_ref, gn1_ref, gn2_ref, proj, ctx, att_sem, d_ctx, d_proj, got, own, stage, from_core, from_y, from_z,
+         out_ref, dx_ref, gq_ref, gk_ref, gv_ref, go_ref, gn1_ref, gn2_ref, proj, ctx, att_sem, d_ctx, d_proj, mats, got, own, stage, from_core, from_y, from_z,
          own_sem, side_z, side_y, sz_send, sz_recv, sy_send, sy_recv, g_recv, g_core, g_y, g_z, s_core, r_core, s_y, r_y, s_z, r_z) = refs
     tokens, dim = own.shape[1], own.shape[2]
     half = w1_ref.shape[0]
@@ -210,6 +210,12 @@
     along_z(0, start)
     gather_to_y(0, me).start()
     gather_to_core(0, me).start()
+    gains = got[me, tokens:, :].astype(F32)
+    attention = Attention(got if backward else mats, proj, ctx, x_ref, gains[choices:choices + 1], gains[choices + 1:choices + 2], head_dim)
+    weights = attention.copies(wq_ref, wk_ref, wv_ref, wo_ref, att_sem)
+    if not backward:
+        for copy in weights:
+            copy.start()
 
     def pass_on(n):
         block = at(column(n), y, c)
@@ -423,6 +429,15 @@
         at_steps(step, at_end, ((1, 0, 1), (2, 0, 2), (3, 0, 3), (4, 1, 3), (5, 1, 2), (6, 1, 1)), lambda across, n: side_chain(across, n, start))
         at_steps(step, inside, ((4, 0, 2), (5, 0, 3), (6, 0, 1), (6, 1, 3), (7, 1, 2), (7, 1, 1)), side_join)
 
+        if not backward:
+            @pl.when(step == 1)
+            def _():
+                attention.heads()
+
+            @pl.when(step == 2)
+            def _():
+                pull_output()
+
         @pl.when(step == 6)
         def _():
             take_y(3)
@@ -433,41 +448,7 @@
 
         return carry
 
-    lax.fori_loop(0, 8, step_body, 0)
-    if backward:
-        stores = [pltpu.make_async_copy(acc, ref, store_sem.at[i]) for i, (acc, ref) in enumerate(((acc1, gw1_ref), (acc2, gw2_ref), (acc3, gw3_ref)))]
-        for store in stores:
-            store.start()
-
-    for n in range(4):
-        along_z(n, sent)
-        gather_to_y(n, me).wait_send()
-    for slot in range(8):
-        gather_to_core(slot, me).wait_send()
-    gains = got[me, tokens:, :].astype(F32)
-    attention = Attention(got, proj, ctx, x_ref, gains[choices:choices + 1], gains[choices + 1:choices + 2], head_dim)
-    weights = attention.copies(wq_ref, wk_ref, wv_ref, wo_ref, att_sem)
-    for copy in weights:
-        copy.start()
-
-    def join(n):
-        @pl.when(inside)
-        def _():
-            take_z(n, column(n))
-            chain(n, start)
-
-    def pass_sum(n):
-        take_y(n)
-
-        @pl.when(at_end)
-        def _():
-            chain(n, start)
-
-    if not backward:
-        for copy in weights:
-            copy.wait()
-        attention.project()
-        attention.heads()
+    def pull_output():
         hid = attention.hidden()
         d_norm, gn2_ref[...] = attention.norm_pull(hid.astype(F32), attention.gain_2, du_ref[...].astype(F32))
         d_hid = (dy_ref[...].astype(F32) + d_norm.astype(F32)).astype(BF16)
@@ -476,21 +457,52 @@
             d_ctx[:, i * attention.chunk:(i + 1) * attention.chunk] = mm_nt(d_hid, attention.weight(4 + i)).astype(BF16)
         for i in range(4):
             go_ref[pl.ds(i * attention.chunk, attention.chunk), :] = mm_tn(attention.part(ctx[...], i), d_hid).astype(BF16)
-    join(3)
-    if backward:
+
+    if not backward:
         for copy in weights:
             copy.wait()
         attention.project()
+    lax.fori_loop(0, 8, step_body, 0)
+    if backward:
+        stores = [pltpu.make_async_copy(acc, ref, store_sem.at[i]) for i, (acc, ref) in enumerate(((acc1, gw1_ref), (acc2, gw2_ref), (acc3, gw3_ref)))]
+        for store in stores:
+            store.start()
+
+    for n in range(4):
+        along_z(n, sent)
+        gather_to_y(n, me).wait_send()
+    for slot in range(8):
+        gather_to_core(slot, me).wait_send()
+    if backward:
+        for copy in weights:
+            copy.start()
+
+    def join(n):
+        @pl.when(inside)
+        def _():
+            take_z(n, column(n))
+            chain(n, start)
+
+    def pass_sum(n):
+        take_y(n)
+
+        @pl.when(at_end)
+        def _():
+            chain(n, start)
+
+    join(3)
     pass_sum(2)
-    join(2)
-    if backward:
+    if backward:
+        for copy in weights:
+            copy.wait()
+        attention.project()
         attention.heads()
     else:
         attention.pull_heads(d_ctx, d_proj)
+    join(2)
     side_gather(1)
     side_cross().start()
     pass_sum(1)
-    join(1)
     kv = attention.kv
     if backward:
         hid = attention.hidden()
@@ -503,6 +515,8 @@
             gq_ref[block, :] = mm_tn(attention.part(rows, i), d_proj[:, :dim]).astype(BF16)
             gk_ref[block, :] = mm_tn(attention.part(rows, i), d_proj[:, dim:dim + kv]).astype(BF16)
             gv_ref[block, :] = mm_tn(attention.part(rows, i), d_proj[:, dim + kv:]).astype(BF16)
+    join(1)
+    if not backward:
         pulled = [mm_nt(d_proj[:, :dim], attention.weight(i)) + mm_nt(d_proj[:, dim:], attention.weight(8 + i)) for i in range(4)]
         d_rows = jnp.concatenate(pulled, axis=1).astype(BF16).astype(F32)
         d_x, gn1_ref[...] = attention.norm_pull(x_ref[...].astype(F32), attention.gain_1, d_rows)
@@ -549,7 +563,7 @@
         dma((16,)),
     ]
     if not backward:
-        scratch += [pltpu.VMEM(block, BF16), pltpu.VMEM((tokens, 2 * dim), BF16)]
+        scratch += [pltpu.VMEM(block, BF16), pltpu.VMEM((tokens, 2 * dim), BF16), pltpu.VMEM((12, dim // 4, dim), BF16)]
     scratch += [
         pltpu.VMEM((16,) + rows.shape, BF16),
         pltpu.VMEM((8,) + block, F32),

time: 337 us -> 327 us (0.970)
  Pallas kernels: 296 us -> 286 us
    pallas_call x2, Pallas kernels: 296 us -> 286 us  [exchange(): pl.pallas_call(functools.partial(exchange_kernel, backward, head_dim, cho...]
where the time goes in v6:
time: 327 us; the launch traced here: 326 us
  Pallas kernels  286 us (87%)
  local copies, waits for them, and re-layouts  28.1 us (9%)
  other arithmetic  11.5 us (4%)
    pallas_call x2, Pallas kernels, exchange(): pl.pallas_call(functools.partial(exchange_kernel, backward, head_dim, cho...  286 us
    unnamed x30, local copies, waits for them, and re-layouts  12.8 us

profile of v6, /device:TPU:0, one launch (start us, length us, event | category | flops | bytes accessed | tf_op | source)
XLA Modules:
  0.0 326.2 jit_solution(3765850020132302633)
XLA Ops:
  0.6 0.7 broadcast_in_dim.9
  2.0 0.7 convert_bitcast_fusion.2
  2.7 0.7 fusion.11
  3.4 0.7 convert_bitcast_fusion
  4.1 0.7 fusion.13
  4.8 1.9 fusion.2.refs_0_
  6.7 4.0 %copy.36.refs_6_.refs_5_ = bf16[1024,1024]{1,0:T(8,128)(2,1)} copy(bf16[1024,1024]{0,1:T(8,128)(2,1)} %bitcast.25) | data formatting | bytes 4194304 | tf_op jit(solution)/shard_map/reshape | solution.py:628
  10.8 1.3 copy.37.refs_7_.refs_6_
  12.1 1.3 copy.38.refs_8_.refs_7_
  13.4 147.5 %exchange_b.1 = (bf16[256,1024]{1,0:T(8,128)(2,1)}, f32[2,1024,512]{2,1,0:T(8,128)}, f32[2,512,1024]{2,1,0:T(8,128)}, f32[2,1024,512]{2,1,0:T(8,128)}, bf16[256,...) custom-call(bf16[272,1024]{1,0:T(8,128)(2,1)} %fusion.2.refs_0_, bf16[2,2048,1024]{2,1,0:T(8,128)(2,1)} %refs_1_.2, ...), custom_call_target="tpu_custom_call" | custom-call | tf_op jit(solution)/shard_map/exchange_b/pallas_call | solution.py:599
  160.9 1.9 fusion.3.refs_0_
  162.8 138.4 %exchange_a.1 = (f32[256,1024]{1,0:T(8,128)}, bf16[256,1024]{1,0:T(8,128)(2,1)}, bf16[1024,1024]{1,0:T(8,128)(2,1)}, bf16[1024,512]{1,0:T(8,128)(2,1)}, bf16[102...) custom-call(bf16[272,1024]{1,0:T(8,128)(2,1)} %fusion.3.refs_0_, ...), custom_call_target="tpu_custom_call" | custom-call | tf_op jit(solution)/shard_map/exchange_a/pallas_call | solution.py:599
  301.2 2.3 add_convert_fusion
  303.5 3.0 copy.42
  306.5 2.7 copy.43
  309.2 1.6 copy.44
  310.8 0.7 copy-done.3
  311.5 2.6 convert.4
  314.1 0.8 copy.51
  315.6 2.1 copy.52
  317.7 1.6 copy-done.1
  319.3 2.1 copy.53
  321.4 1.6 copy-done
  323.0 2.0 copy.54
  (25 shorter events, 2.6 us)
Async XLA Ops:
  6.7 4.0 %copy-start.6 = (bf16[1024,8,64]{0,2,1:T(8,128)(2,1)S(1)}, bf16[1024,8,64]{0,2,1:T(8,128)(2,1)}, u32[]{:S(2)}) copy-start(bf16[1024,8,64]{0,2,1:T(8,128)(2,1)} %param.32) | copy-start | bytes 3145732
  10.8 1.3 copy-start.7
  162.8 138.4 %copy-start.9 = (bf16[256,1024]{1,0:T(8,128)(2,1)S(1)}, bf16[256,1024]{1,0:T(8,128)(2,1)}, u32[]{:S(2)}) copy-start(bf16[256,1024]{1,0:T(8,128)(2,1)} %get-tuple-element.25) | copy-start | bytes 1572868
  301.2 2.4 copy-start.4
  306.5 2.7 copy-start.5
  309.2 2.3 copy-start.3
  311.5 2.6 copy-start.8
  311.5 4.1 %copy-start.2 = (f32[2,1024,512]{2,1,0:T(8,128)S(1)}, f32[2,1024,512]{2,1,0:T(8,128)}, u32[]{:S(2)}) copy-start(f32[2,1024,512]{2,1,0:T(8,128)} %get-tuple-element.69) | copy-start | bytes 12582916
  315.6 3.7 %copy-start.1 = (f32[2,512,1024]{2,1,0:T(8,128)S(1)}, f32[2,512,1024]{2,1,0:T(8,128)}, u32[]{:S(2)}) copy-start(f32[2,512,1024]{2,1,0:T(8,128)} %get-tuple-element.70) | copy-start | bytes 12582916
  319.3 3.7 %copy-start = (f32[2,1024,512]{2,1,0:T(8,128)S(1)}, f32[2,1024,512]{2,1,0:T(8,128)}, u32[]{:S(2)}) copy-start(f32[2,1024,512]{2,1,0:T(8,128)} %get-tuple-element.71) | copy-start | bytes 12582916
  323.0 2.0 copy-start.11
  323.0 2.6 copy-start.10

commit v7 on v6

--- a/solution.py
+++ b/solution.py
@@ -140,7 +140,7 @@
          out_ref, gw1_ref, gw2_ref, gw3_ref, h_ref, norm_ref, proj, ctx, att_sem, got, own, stage, from_core, from_y, from_z, saved, acc1, acc2, acc3,
          own_sem, load_sem, store_sem, side_z, side_y, sz_send, sz_recv, sy_send, sy_recv, g_recv, g_core, g_y, g_z, s_core, r_core, s_y, r_y, s_z, r_z) = refs
     else:
-        (rows_ref, w1_ref, w3_ref, w2_ref, x_ref, wq_ref, wk_ref, wv_ref, wo_ref, dy_ref, du_ref,
+        (rows_ref, w1_ref, w3_ref, w2_ref, x_ref, wq_ref, wk_ref, wv_ref, wo_ref, dy_ref, du_ref, base_ref,
          out_ref, dx_ref, gq_ref, gk_ref, gv_ref, go_ref, gn1_ref, gn2_ref, proj, ctx, att_sem, d_ctx, d_proj, mats, got, own, stage, from_core, from_y, from_z,
          own_sem, side_z, side_y, sz_send, sz_recv, sy_send, sy_recv, g_recv, g_core, g_y, g_z, s_core, r_core, s_y, r_y, s_z, r_z) = refs
     tokens, dim = own.shape[1], own.shape[2]
@@ -534,7 +534,8 @@
     def _():
         take_z(0, 4)
 
-    out_ref[...] = own[0].astype(out_ref.dtype)
+    total = own[0] if backward else base_ref[...].astype(F32) + own[0]
+    out_ref[...] = total.astype(BF16)
     for n in (3, 2, 1):
         chain(n, sent)
         side_chain(0, n, sent)
@@ -591,8 +592,8 @@
     else:
         scratch += [dma(())]
         operands = (rows, w_1, w_3, w_2) + sequence
-        in_specs = [any_spec] + [vmem_spec] * 4 + [any_spec] * 4 + [vmem_spec] * 2
-        out_shape = [jax.ShapeDtypeStruct(block, F32), jax.ShapeDtypeStruct(block, BF16)]
+        in_specs = [any_spec] + [vmem_spec] * 4 + [any_spec] * 4 + [vmem_spec] * 3
+        out_shape = [jax.ShapeDtypeStruct(block, BF16)] * 2
         out_shape += [jax.ShapeDtypeStruct(shape, BF16) for shape in (model, narrow, narrow, model)]
         out_shape += [jax.ShapeDtypeStruct((1, dim), F32)] * 2
         out_specs = [vmem_spec] * 8
@@ -627,8 +628,7 @@
         head_dim = w_q.shape[2]
         layer = (w_q.reshape(model_dim, -1), w_k.reshape(model_dim, -1), w_v.reshape(model_dim, -1), w_o.reshape(-1, model_dim))
         du_rows, grad_w1, grad_w2, grad_w3, h_a, u_a = exchange(True, with_routing(dy_b, eid_b, slot_b, gate_b), weights, tokens, head_dim, eid_b.shape[1], (x_a,) + layer, u_b)
-        mixed, dx_b, g_q, g_k, g_v, g_o, g_n1, g_n2 = exchange(False, with_routing(u_a, eid_a, slot_a, gate_a), weights, tokens, head_dim, eid_a.shape[1], (x_b,) + layer + (dy_b, du_rows))
-        y_a = (h_a.astype(jnp.float32) + mixed).astype(jnp.bfloat16)
+        y_a, dx_b, g_q, g_k, g_v, g_o, g_n1, g_n2 = exchange(False, with_routing(u_a, eid_a, slot_a, gate_a), weights, tokens, head_dim, eid_a.shape[1], (x_b,) + layer + (dy_b, du_rows, h_a))
         g_q, g_k, g_v, g_o = (grad.astype(jnp.float32).reshape(weight.shape) for grad, weight in ((g_q, w_q), (g_k, w_k), (g_v, w_v), (g_o, w_o)))
         g_n1, g_n2 = g_n1[0], g_n2[0]
         return (y_a, dx_b, grad_w1, grad_w2, grad_w3, g_q[None], g_k[None], g_v[None], g_o[None], g_n1[None], g_n2[None])

time: 327 us -> 325 us (level)
    unnamed x30 -> x31, local copies, waits for them, and re-layouts: 12.8 us -> 13 us
where the time goes in v7:
time: 325 us; the launch traced here: 324 us
  Pallas kernels  286 us (88%)
  local copies, waits for them, and re-layouts  28.4 us (9%)
  other arithmetic  9.21 us (3%)
    pallas_call x2, Pallas kernels, exchange(): pl.pallas_call(functools.partial(exchange_kernel, backward, head_dim, cho...  286 us
    unnamed x31, local copies, waits for them, and re-layouts  13 us

profile of v7, /device:TPU:0, one launch (start us, length us, event | category | flops | bytes accessed | tf_op | source)
XLA Modules:
  0.0 324.3 jit_solution(9420460079009981114)
XLA Ops:
  0.6 0.7 broadcast_in_dim.9
  2.0 0.7 convert_bitcast_fusion.2
  2.7 0.7 fusion.11
  3.4 0.7 convert_bitcast_fusion
  4.1 0.7 fusion.13
  4.8 1.9 fusion.2.refs_0_
  6.7 4.0 %copy.36.refs_6_.refs_5_ = bf16[1024,1024]{1,0:T(8,128)(2,1)} copy(bf16[1024,1024]{0,1:T(8,128)(2,1)} %bitcast.25) | data formatting | bytes 4194304 | tf_op jit(solution)/shard_map/reshape | solution.py:629
  10.8 1.3 copy.37.refs_7_.refs_6_
  12.1 1.3 copy.38.refs_8_.refs_7_
  13.4 147.5 %exchange_b.1 = (bf16[256,1024]{1,0:T(8,128)(2,1)}, f32[2,1024,512]{2,1,0:T(8,128)}, f32[2,512,1024]{2,1,0:T(8,128)}, f32[2,1024,512]{2,1,0:T(8,128)}, bf16[256,...) custom-call(bf16[272,1024]{1,0:T(8,128)(2,1)} %fusion.2.refs_0_, bf16[2,2048,1024]{2,1,0:T(8,128)(2,1)} %refs_1_.2, ...), custom_call_target="tpu_custom_call" | custom-call | tf_op jit(solution)/shard_map/exchange_b/pallas_call | solution.py:600
  160.9 1.9 fusion.3.refs_0_
  162.8 138.4 %exchange_a.1 = (bf16[256,1024]{1,0:T(8,128)(2,1)}, bf16[256,1024]{1,0:T(8,128)(2,1)}, bf16[1024,1024]{1,0:T(8,128)(2,1)}, bf16[1024,512]{1,0:T(8,128)(2,1)}, bf...) custom-call(bf16[272,1024]{1,0:T(8,128)(2,1)} %fusion.3.refs_0_, ...), custom_call_target="tpu_custom_call" | custom-call | tf_op jit(solution)/shard_map/exchange_a/pallas_call | solution.py:600
  301.3 4.2 %copy.42 = f32[1024,1024]{0,1:T(8,128)} copy(bf16[1024,1024]{1,0:T(8,128)(2,1)} %get-tuple-element.33) | data formatting | bytes 6291456 | tf_op jit(solution)/shard_map/broadcast_in_dim;reshape | solution.py:634
  305.5 1.6 copy.43
  307.1 1.6 copy.44
  308.7 0.7 copy-done.3
  309.4 2.6 convert.4
  312.0 0.8 copy.52
  312.8 0.8 copy.53
  313.7 2.1 copy.54
  315.8 1.6 copy-done.1
  317.4 2.1 copy.55
  319.5 1.6 copy-done
  321.1 2.0 copy.56
  (25 shorter events, 1.9 us)
Async XLA Ops:
  6.7 4.0 %copy-start.6 = (bf16[1024,8,64]{0,2,1:T(8,128)(2,1)S(1)}, bf16[1024,8,64]{0,2,1:T(8,128)(2,1)}, u32[]{:S(2)}) copy-start(bf16[1024,8,64]{0,2,1:T(8,128)(2,1)} %param.32) | copy-start | bytes 3145732
  10.8 1.3 copy-start.7
  301.3 4.2 %copy-start.5 = (bf16[1024,512]{1,0:T(8,128)(2,1)S(1)}, bf16[1024,512]{1,0:T(8,128)(2,1)}, u32[]{:S(2)}) copy-start(bf16[1024,512]{1,0:T(8,128)(2,1)} %get-tuple-element.34) | copy-start | bytes 3145732
  305.5 1.6 copy-start.4
  307.1 2.3 copy-start.3
  309.4 2.6 copy-start.9
  309.4 3.4 %copy-start.8 = (bf16[256,1024]{1,0:T(8,128)(2,1)S(1)}, bf16[256,1024]{1,0:T(8,128)(2,1)}, u32[]{:S(2)}) copy-start(bf16[256,1024]{1,0:T(8,128)(2,1)} %get-tuple-element.68) | copy-start | bytes 1572868
  309.4 4.2 %copy-start.2 = (f32[2,1024,512]{2,1,0:T(8,128)S(1)}, f32[2,1024,512]{2,1,0:T(8,128)}, u32[]{:S(2)}) copy-start(f32[2,1024,512]{2,1,0:T(8,128)} %get-tuple-element.69) | copy-start | bytes 12582916
  313.7 3.7 %copy-start.1 = (f32[2,512,1024]{2,1,0:T(8,128)S(1)}, f32[2,512,1024]{2,1,0:T(8,128)}, u32[]{:S(2)}) copy-start(f32[2,512,1024]{2,1,0:T(8,128)} %get-tuple-element.70) | copy-start | bytes 12582916
  317.4 3.7 %copy-start = (f32[2,1024,512]{2,1,0:T(8,128)S(1)}, f32[2,1024,512]{2,1,0:T(8,128)}, u32[]{:S(2)}) copy-start(f32[2,1024,512]{2,1,0:T(8,128)} %get-tuple-element.71) | copy-start | bytes 12582916
  321.1 2.0 copy-start.11
  321.1 2.6 copy-start.10
